TPU v7x, 128 devices: a whole 4x4x4 slice. The times are simulated.
128 devices in a mesh: dp: 1, tp: 2 (over core), cp: 64 (over z, y, x).
Axes of the slice: x: 4, y: 4, z: 4, core: 2. Of those that a mesh axis runs over, the one named last changes fastest.
Arguments:
- tokens_in: bfloat16 [16384, 3072], P(('dp', 'cp', 'tp'))
- grad_out: bfloat16 [16384, 3072], P(('dp', 'cp', 'tp'))
- w_query: bfloat16 [3072, 3072], P(None, 'tp')
- w_key: bfloat16 [3072, 1024], P(None, 'tp')
- w_value: bfloat16 [3072, 1024], P(None, 'tp')
- w_out: bfloat16 [3072, 3072], P('tp')
Outputs:
- output 1: bfloat16 [16384, 3072], P(('dp', 'cp', 'tp'))
- output 2: bfloat16 [16384, 3072], P(('dp', 'cp', 'tp'))
All inputs are finite; a program needn't handle non-finite values.
Results may differ from a plain program's by a relative error of at most 0.00949005.
Values are sent between devices in bfloat16 or wider.
A program may use at most 1 GiB of HBM per device.

v0:
```python
import jax
import jax.numpy as jnp
from jax import lax
from jax.sharding import PartitionSpec as P

HEAD_DIM = 128


def block_rows(piece_rows, key_rows, head_count):
    budget = max(1, (1 << 22) // (key_rows * head_count))
    row_count = 8
    for candidate in (16, 32, 64, 128):
        if candidate <= budget and piece_rows % candidate == 0:
            row_count = candidate
    return row_count


def fold_positions(row_ids, seq_loc, cp_size):
    piece_rows = seq_loc // 2
    shard_idx = row_ids // seq_loc
    within = row_ids % seq_loc
    piece_id = jnp.where(within < piece_rows, shard_idx, 2 * cp_size - 1 - shard_idx)
    return piece_id * piece_rows + within % piece_rows


def dot_transposed(left, right):
    return lax.dot_general(left, right, (((1,), (1,)), ((), ())), preferred_element_type=jnp.float32)


def solution(mesh):
    cp_size = mesh.shape['cp']
    row_spec = P(('dp', 'cp', 'tp'), None)

    def local_step(x_blk, dy_blk, w_query, w_key, w_value, w_out):
        cp_rank = lax.axis_index('cp')
        x_loc = lax.all_gather(x_blk, 'tp', axis=0, tiled=True)
        seq_loc = x_loc.shape[0]
        seq_all = seq_loc * cp_size
        piece_rows = seq_loc // 2
        heads_q = w_query.shape[1] // HEAD_DIM
        heads_kv = w_key.shape[1] // HEAD_DIM
        group_size = heads_q // heads_kv
        score_scale = HEAD_DIM ** -0.5
        query_loc = jnp.dot(x_loc, w_query, preferred_element_type=jnp.float32).astype(jnp.bfloat16).reshape(seq_loc, heads_kv, group_size, HEAD_DIM)
        keys_loc = jnp.dot(x_loc, w_key, preferred_element_type=jnp.float32).astype(jnp.bfloat16).reshape(seq_loc, heads_kv, HEAD_DIM)
        values_loc = jnp.dot(x_loc, w_value, preferred_element_type=jnp.float32).astype(jnp.bfloat16).reshape(seq_loc, heads_kv, HEAD_DIM)
        keys_all = lax.all_gather(keys_loc, 'cp', axis=0, tiled=True)
        values_all = lax.all_gather(values_loc, 'cp', axis=0, tiled=True)
        dy_loc = lax.all_gather(dy_blk, 'tp', axis=0, tiled=True)
        d_out = dot_transposed(dy_loc, w_out).astype(jnp.bfloat16).reshape(seq_loc, heads_kv, group_size, HEAD_DIM)
        key_pos = fold_positions(jnp.arange(seq_all, dtype=jnp.int32), seq_loc, cp_size)
        query_pos = fold_positions(cp_rank * seq_loc + jnp.arange(seq_loc, dtype=jnp.int32), seq_loc, cp_size)
        blk_rows = block_rows(piece_rows, seq_all, heads_q)
        block_count = seq_loc // blk_rows

        def block_step(acc_pair, blk_in):
            dk_acc, dv_acc = acc_pair
            q_blk, do_blk, pos_blk = blk_in
            scores = jnp.einsum('qhgd,khd->hgqk', q_blk, keys_all, preferred_element_type=jnp.float32) * score_scale
            allowed = pos_blk[:, None] >= key_pos[None, :]
            scores = jnp.where(allowed, scores, -jnp.inf)
            log_norm = jax.nn.logsumexp(scores, axis=-1, keepdims=True)
            prob_bf = jnp.exp(scores - log_norm).astype(jnp.bfloat16)
            out_blk = jnp.einsum('hgqk,khd->qhgd', prob_bf, values_all, preferred_element_type=jnp.float32).astype(jnp.bfloat16)
            row_delta = jnp.einsum('qhgd,qhgd->hgq', do_blk, out_blk, preferred_element_type=jnp.float32)
            d_prob = jnp.einsum('qhgd,khd->hgqk', do_blk, values_all, preferred_element_type=jnp.float32)
            d_score = (prob_bf.astype(jnp.float32) * (d_prob - row_delta[..., None])).astype(jnp.bfloat16)
            dq_blk = (jnp.einsum('hgqk,khd->qhgd', d_score, keys_all, preferred_element_type=jnp.float32) * score_scale).astype(jnp.bfloat16)
            dk_acc = dk_acc + jnp.einsum('hgqk,qhgd->khd', d_score, q_blk, preferred_element_type=jnp.float32) * score_scale
            dv_acc = dv_acc + jnp.einsum('hgqk,qhgd->khd', prob_bf, do_blk, preferred_element_type=jnp.float32)
            return (dk_acc, dv_acc), (out_blk, dq_blk)

        zeros_kv = jnp.zeros((seq_all, heads_kv, HEAD_DIM), jnp.float32)
        blk_inputs = (query_loc.reshape(block_count, blk_rows, heads_kv, group_size, HEAD_DIM), d_out.reshape(block_count, blk_rows, heads_kv, group_size, HEAD_DIM), query_pos.reshape(block_count, blk_rows))
        (dk_part, dv_part), (out_blocks, dq_blocks) = lax.scan(block_step, (zeros_kv, zeros_kv), blk_inputs)
        attn_out = out_blocks.reshape(seq_loc, heads_q * HEAD_DIM)
        d_query = dq_blocks.reshape(seq_loc, heads_q * HEAD_DIM)
        y_part = jnp.dot(attn_out, w_out, preferred_element_type=jnp.float32)
        y_blk = lax.psum_scatter(y_part, 'tp', scatter_dimension=0, tiled=True).astype(jnp.bfloat16)
        dk_own = lax.psum_scatter(dk_part, 'cp', scatter_dimension=0, tiled=True).astype(jnp.bfloat16).reshape(seq_loc, heads_kv * HEAD_DIM)
        dv_own = lax.psum_scatter(dv_part, 'cp', scatter_dimension=0, tiled=True).astype(jnp.bfloat16).reshape(seq_loc, heads_kv * HEAD_DIM)
        dx_part = dot_transposed(d_query, w_query) + dot_transposed(dk_own, w_key) + dot_transposed(dv_own, w_value)
        dx_blk = lax.psum_scatter(dx_part, 'tp', scatter_dimension=0, tiled=True).astype(jnp.bfloat16)
        return y_blk, dx_blk

    return jax.shard_map(local_step, mesh=mesh, in_specs=(row_spec, row_spec, P(None, 'tp'), P(None, 'tp'), P(None, 'tp'), P('tp', None)), out_specs=(row_spec, row_spec), check_vma=False)
```

profile of v0, /device:TPU:1, one launch (start us, length us, event | category | flops | bytes accessed | tf_op | source)
XLA Modules:
  0.0 2999.1 jit_solution(14075918990267850602)
XLA Ops:
  8.7 17.1 all-gather.5.cloned.1.call-done
  68.5 81.2 %all-gather.11.cloned.1.call-done = bf16[16384,4,128]{2,0,1:T(8,128)(2,1)} async-done(((bf16[256,4,128]{2,0,1:T(8,128)(2,1)}), bf16[16384,4,128]{2,0,1:T(8,128)(2,1)}) %all-gather.11.cloned.1.call-update) | async-done | bytes 16777232 | tf_op jit(solution)/shard_map/all_gather | solution.py:48
  149.7 107.2 %all-gather.7.cloned.1.call-done = bf16[16384,4,128]{2,0,1:T(8,128)(2,1)} async-done(((bf16[256,4,128]{2,0,1:T(8,128)(2,1)}), bf16[16384,4,128]{2,0,1:T(8,128)(2,1)}) %all-gather.7.cloned.1.call-update) | async-done | bytes 16777232 | tf_op jit(solution)/shard_map/all_gather | solution.py:47
  256.9 1807.4 %while.17 = (s32[]{:T(128)}, f32[16384,4,128]{0,2,1:T(8,128)}, f32[16384,4,128]{0,2,1:T(8,128)}, bf16[16,16,4,3,128]{4,1,3,2,0:T(8,128)(2,1)}, bf16[16,16,4,3,12...) while((s32[]{:T(128)}, f32[16384,4,128]{0,2,1:T(8,128)}, ...), condition=%wide.region_3.4_spmd.clone, body=%wide.region_0.3_spmd.clone.sunk | while | flops 4909277696 | bytes 284222048 | solution.py:75
  295.7 12.3 fusion.112
  318.9 14.5 bitcast_add_fusion.4
  333.4 14.5 bitcast_add_fusion.5
  410.0 26.2 bitcast_add_fusion.4
  436.2 26.2 bitcast_add_fusion.5
  524.4 26.2 bitcast_add_fusion.4
  550.6 26.2 bitcast_add_fusion.5
  638.8 26.2 bitcast_add_fusion.4
  665.0 26.2 bitcast_add_fusion.5
  730.0 12.3 fusion.112
  753.3 26.2 bitcast_add_fusion.4
  779.5 26.2 bitcast_add_fusion.5
  844.4 12.3 fusion.112
  867.7 26.2 bitcast_add_fusion.4
  893.9 26.2 bitcast_add_fusion.5
  958.8 12.3 fusion.112
  982.1 26.2 bitcast_add_fusion.4
  1008.3 26.2 bitcast_add_fusion.5
  1096.5 26.2 bitcast_add_fusion.4
  1122.7 26.2 bitcast_add_fusion.5
  1211.0 26.2 bitcast_add_fusion.4
  1237.2 26.2 bitcast_add_fusion.5
  1325.4 26.2 bitcast_add_fusion.4
  1351.6 26.2 bitcast_add_fusion.5
  1416.5 12.3 fusion.112
  1439.8 26.2 bitcast_add_fusion.4
  1466.0 26.2 bitcast_add_fusion.5
  1554.2 26.2 bitcast_add_fusion.4
  1580.4 26.2 bitcast_add_fusion.5
  1645.4 12.3 fusion.112
  1668.7 26.2 bitcast_add_fusion.4
  1694.9 26.2 bitcast_add_fusion.5
  1759.8 12.3 fusion.112
  1783.1 26.2 bitcast_add_fusion.4
  1809.3 26.2 bitcast_add_fusion.5
  1874.2 12.3 fusion.112
  1897.5 26.2 bitcast_add_fusion.4
  1923.7 26.2 bitcast_add_fusion.5
  2011.9 26.2 bitcast_add_fusion.4
  2038.1 26.2 bitcast_add_fusion.5
  2093.3 387.6 %reduce-scatter.7.cloned.1.call-done = f32[256,4,128]{0,2,1:T(8,128)} async-done(((f32[16384,4,128]{0,2,1:T(8,128)}), f32[256,4,128]{0,2,1:T(8,128)}) %reduce-scatter.7.cloned.1.call-update) | async-done | bytes 524304 | tf_op jit(solution)/shard_map/reduce_scatter | solution.py:80
  2481.9 447.9 %reduce-scatter.9.cloned.1.call-done = f32[256,4,128]{0,2,1:T(8,128)} async-done(((f32[16384,4,128]{0,2,1:T(8,128)}), f32[256,4,128]{0,2,1:T(8,128)}) %reduce-scatter.9.cloned.1.call-update) | async-done | bytes 524304 | tf_op jit(solution)/shard_map/reduce_scatter | solution.py:81
  2936.7 36.6 %reduce-scatter.5.cloned.1.call-done = f32[128,3072]{1,0:T(8,128)} async-done(((f32[256,3072]{1,0:T(8,128)}), f32[128,3072]{1,0:T(8,128)}) %reduce-scatter.5.cloned.1.call-update) | async-done | bytes 1572880 | tf_op jit(solution)/shard_map/reduce_scatter | solution.py:79
  2975.7 14.2 reduce-scatter.11.cloned.1.call-done
  (232 shorter events, 979.9 us)
Async XLA Ops:
  7.2 22.8 copy-start
  7.2 18.6 all-gather.5.cloned.1.call-start
  7.9 33.3 %all-gather.9.cloned.1.call-start = ((), (), s32[]{:S(2)}) async-start(), calls=%async_computation.6 | async-start | bytes 2359296 | tf_op jit(solution)/shard_map/all_gather | solution.py:49
  8.7 141.0 %all-gather.11.cloned.1.call-start = ((), (), s32[]{:S(2)}) async-start(), calls=%async_computation.7 | async-start | bytes 17039360 | tf_op jit(solution)/shard_map/all_gather | solution.py:48
  29.9 227.0 %all-gather.7.cloned.1.call-start = ((), (), s32[]{:S(2)}) async-start(), calls=%async_computation.5 | async-start | bytes 17039360 | tf_op jit(solution)/shard_map/all_gather | solution.py:47
  33.1 2447.8 %reduce-scatter.7.cloned.1.call-start = ((), (), s32[]{:S(2)}) async-start(), calls=%async_computation.9 | async-start | bytes 34078720 | tf_op jit(solution)/shard_map/reduce_scatter | solution.py:80
  2064.3 865.5 %reduce-scatter.9.cloned.1.call-start = ((), (), s32[]{:S(2)}) async-start(), calls=%async_computation.10 | async-start | bytes 34078720 | tf_op jit(solution)/shard_map/reduce_scatter | solution.py:81
  2064.9 908.4 %reduce-scatter.5.cloned.1.call-start = ((), (), s32[]{:S(2)}) async-start(), calls=%async_computation.8 | async-start | bytes 4718592 | tf_op jit(solution)/shard_map/reduce_scatter | solution.py:79
  2079.0 910.8 %reduce-scatter.11.cloned.1.call-start = ((), (), s32[]{:S(2)}) async-start(), calls=%async_computation.11 | async-start | bytes 4718592 | tf_op jit(solution)/shard_map/reduce_scatter | solution.py:83
  2929.8 4.2 copy-start.1
Sparse Core Ops, SparseCore 0:
  9.6 16.0 all-gather.4
  27.4 13.7 all-gather.8
  44.1 105.5 all-gather.10
  152.4 104.4 all-gather.6
  2064.5 416.3 reduce-scatter.6
  2483.1 446.6 reduce-scatter.8
  2932.2 41.0 reduce-scatter.4
  2975.6 14.1 reduce-scatter.10
where the time goes:
time: 3000 us
  matrix products  1590 us (53%)
  waiting for transfers between devices  1100 us (37%)
  other arithmetic  256 us (9%)
  local copies, waits for them, and re-layouts  35.3 us (1%)
    reduce_scatter x1, waiting for transfers between devices, local_step(): lax.psum_scatter(dv_part, 'cp', scatter_dimension=0, tiled=True)  448 us
    dot_general x16, matrix products, block_step(): jnp.einsum('hgqk,qhgd->khd', d_score, q_blk, preferred_element_type=jnp.f...  407 us
    dot_general x16, matrix products, block_step(): jnp.einsum('hgqk,qhgd->khd', prob_bf, do_blk, preferred_element_type=jnp....  407 us
    reduce_scatter x1, waiting for transfers between devices, local_step(): lax.psum_scatter(dk_part, 'cp', scatter_dimension=0, tiled=True)  388 us
    dot_general x16, matrix products, block_step(): jnp.einsum('qhgd,khd->hgqk', do_blk, values_all, preferred_element_type=j...  197 us
    dot_general x16, matrix products, block_step(): jnp.einsum('qhgd,khd->hgqk', q_blk, keys_all, preferred_element_type=jnp....  195 us
    dot_general x16, matrix products, block_step(): jnp.einsum('hgqk,khd->qhgd', d_score, keys_all, preferred_element_type=jn...  176 us
    dot_general x16, matrix products, block_step(): jnp.einsum('hgqk,khd->qhgd', prob_bf, values_all, preferred_element_type=...  167 us
  transfers between devices with their start and end apart: 8, of which 8 were waited for; matrix products, arithmetic and copies ran while one was open for 2% of the time, Pallas kernels for 0%

commit v1 on v0

v1 whole, which is shorter than its diff:
```python
import functools

import jax
import jax.numpy as jnp
from jax import lax
from jax.experimental import pallas as pl
from jax.experimental.pallas import tpu as pltpu
from jax.sharding import PartitionSpec as P

HD = 128
S = 16384
G = 3
KT = 512
UQ = 256
C2 = (HD ** -0.5) * 1.4426950408889634
TSC = HD ** -0.5
NEG = float(jnp.finfo(jnp.float32).min)
NINF = -float('inf')
BF = jnp.bfloat16
F32 = jnp.float32
MIB = 2 ** 20


def dg(a, b, ca, cb):
    return lax.dot_general(a, b, (((ca,), (cb,)), ((), ())), preferred_element_type=F32)


def split(c):
    z, y, x = c // 16, (c // 4) % 4, c % 4
    zz, yy = z // 2, y // 2
    xx = ((x + 1) // 2 + 1) % 2
    return (z + zz * (3 - 2 * z), y + yy * (3 - 2 * y), (x // 2 + yy) % 2), (zz, yy, xx)


def chip(grp, head):
    (za, ya, s), (zz, yy, xx) = grp, head
    z = za + zz * (3 - 2 * za)
    y = ya + yy * (3 - 2 * ya)
    hi = (s + yy) % 2
    return z * 16 + y * 4 + hi * (2 + xx) + (1 - hi) * (1 - xx)


def base_unit(grp, k):
    za, ya, s = grp
    return za * 8 + (ya + k * (3 - 2 * ya)) * 2 + s + k * (1 - 2 * s)


def unit_of(i, j):
    return (j // 2) * 32 + (j % 2) * 31 + (1 - 2 * (j % 2)) * i


def flip(grp, mask):
    return tuple(g + (1 - 2 * g) if (mask >> d) & 1 else g for d, g in enumerate(grp))


def quad_block(grp, k, zs, par):
    za, ya, s = grp
    ys = (zs + k) % 2
    z = za + zs * (3 - 2 * za)
    y = ya + ys * (3 - 2 * ya)
    return z * 16 + y * 4 + ((s + ys) % 2) * 2 + par


def dev(c, t):
    return {'tp': t, 'cp': c}


def me():
    c, t = lax.axis_index('cp'), lax.axis_index('tp')
    grp, head = split(c)
    return c, t, grp, head


def rd(start, n):
    return pl.ds(pl.multiple_of(start, n), n)


def greet(c, t, grp, head, cube):
    bar = pltpu.get_barrier_semaphore()
    n = 15
    for hh in range(8):
        for k in range(2):
            cc = chip(grp, (hh // 4, (hh // 2) % 2, hh % 2))

            @pl.when((cc != c) | (t != k))
            def _():
                pl.semaphore_signal(bar, 1, device_id=dev(cc, k), device_id_type=pl.DeviceIdType.MESH)
    if cube:
        for d in range(3):
            pl.semaphore_signal(bar, 1, device_id=dev(chip(flip(grp, 1 << d), head), t), device_id_type=pl.DeviceIdType.MESH)
        n += 3
    pl.semaphore_wait(bar, n)


def rcopy(src, dst, ssem, rsem, cc, k):
    return pltpu.make_async_remote_copy(src_ref=src, dst_ref=dst, send_sem=ssem, recv_sem=rsem, device_id=dev(cc, k), device_id_type=pl.DeviceIdType.MESH)


def send(src, dst, ssem, rsem, cc, k, own):
    @pl.when(own)
    def _():
        pltpu.make_async_copy(src, dst, rsem).start()

    @pl.when(jnp.logical_not(own))
    def _():
        rcopy(src, dst, ssem, rsem, cc, k).start()


def sent(src, dst, ssem, rsem, cc, k, own):
    @pl.when(jnp.logical_not(own))
    def _():
        rcopy(src, dst, ssem, rsem, cc, k).wait_send()


def got(dst, rsem):
    pltpu.make_async_copy(dst, dst, rsem).wait()


def order(it):
    return [(it + r) % 3 for r in range(3)]


def below(dims):
    masks = [0]
    for d in dims:
        masks += [m | (1 << d) for m in masks]
    return masks


VM = pl.BlockSpec(memory_space=pltpu.VMEM)
ANY = pl.BlockSpec(memory_space=pl.ANY)


def params(mib, cid=None):
    kw = {} if cid is None else dict(collective_id=cid, has_side_effects=True)
    return pltpu.CompilerParams(vmem_limit_bytes=mib * MIB, **kw)


def shape(s, d):
    return jax.ShapeDtypeStruct(s, d)


def pair_kernel(x_ref, dy_ref, xo_ref, do_ref, ssem, rsem):
    c, t = lax.axis_index('cp'), lax.axis_index('tp')
    bar = pltpu.get_barrier_semaphore()
    pl.semaphore_signal(bar, 1, device_id=dev(c, 1 - t), device_id_type=pl.DeviceIdType.MESH)
    pl.semaphore_wait(bar, 1)
    n = x_ref.shape[0]
    mine = rd(t * n, n)
    cps = [rcopy(src, dst.at[mine, :], ssem.at[e], rsem.at[e], c, 1 - t) for e, (src, dst) in enumerate(((x_ref, xo_ref), (dy_ref, do_ref)))]
    for cp in cps:
        cp.start()
    xo_ref[mine, :] = x_ref[...]
    do_ref[mine, :] = dy_ref[...]
    for cp in cps:
        cp.wait()


def pair_gather(x, dy):
    n, d = x.shape
    return pl.pallas_call(
        pair_kernel, out_shape=(shape((2 * n, d), x.dtype),) * 2, in_specs=[VM] * 2, out_specs=(VM,) * 2,
        scratch_shapes=[pltpu.SemaphoreType.DMA((2,)), pltpu.SemaphoreType.DMA((2,))],
        compiler_params=params(16, 0), name='pair_gather')(x, dy)


def pair_sum_kernel(y_ref, dx_ref, yo_ref, do_ref, ssem, rsem):
    c, t = lax.axis_index('cp'), lax.axis_index('tp')
    bar = pltpu.get_barrier_semaphore()
    pl.semaphore_signal(bar, 1, device_id=dev(c, 1 - t), device_id_type=pl.DeviceIdType.MESH)
    pl.semaphore_wait(bar, 1)
    n = yo_ref.shape[0]
    other = rd((1 - t) * n, n)
    cps = [rcopy(src.at[other, :], dst, ssem.at[e], rsem.at[e], c, 1 - t) for e, (src, dst) in enumerate(((y_ref, yo_ref), (dx_ref, do_ref)))]
    for cp in cps:
        cp.start()
    for cp in cps:
        cp.wait()


def pair_half(y, dx):
    n, d = y.shape
    return pl.pallas_call(
        pair_sum_kernel, out_shape=(shape((n // 2, d), y.dtype),) * 2, in_specs=[VM] * 2, out_specs=(VM,) * 2,
        scratch_shapes=[pltpu.SemaphoreType.DMA((2,)), pltpu.SemaphoreType.DMA((2,))],
        compiler_params=params(16, 1), name='pair_half')(y, dx)


def spread_kernel(q_ref, do_ref, k_ref, v_ref, qo_ref, doo_ref, ko_ref, vo_ref, ss1, rs1, ss2, rs2, ss3, rs3):
    c, t, grp, head = me()
    zb, yb, xb = head
    b = c
    par = c % 2
    k = (zb + yb) % 2
    greet(c, t, grp, head, True)

    def rows_q(zs, pr, e):
        j = zs + e * (3 - 2 * zs)
        return rd(j * UQ + (pr + e * (1 - 2 * pr)) * 128, 128)

    def rows_k(bb, e):
        return rd((bb + e * (127 - 2 * bb)) * 128, 128)

    def first(fn, kinds):
        for hh in range(4):
            cc = chip(grp, (t, hh // 2, hh % 2))
            own = (cc == c) & (k == t)
            for n in kinds:
                for e in range(2):
                    wide = HD if n < 2 else G * HD
                    src = (k_ref, v_ref, q_ref, do_ref)[n].at[e * 128:(e + 1) * 128, hh * wide:(hh + 1) * wide]
                    dst = (ko_ref, vo_ref, qo_ref, doo_ref)[n].at[rows_k(b, e) if n < 2 else rows_q(zb, par, e), :]
                    fn(src, dst, ss1.at[hh, n, e], rs1.at[zb * 2 + par, n, e], cc, k, own)

    def first_got(kinds):
        for zs in range(2):
            for pr in range(2):
                bb = quad_block(grp, t, zs, pr)
                for n in kinds:
                    for e in range(2):
                        dst = (ko_ref, vo_ref, qo_ref, doo_ref)[n].at[rows_k(bb, e) if n < 2 else rows_q(zs, pr, e), :]
                        got(dst, rs1.at[zs * 2 + pr, n, e])

    first(send, (0, 1))
    first(send, (2, 3))
    first_got((0, 1))

    def part(it, mask, kk):
        r = rd(unit_of(base_unit(flip(grp, mask), kk), it // 2) * UQ, UQ)
        return (ko_ref, vo_ref)[it % 2].at[r, :]

    def hop(it, r, mask):
        d = order(it)[r]
        ref = part(it, mask, t)
        m2 = mask | (1 << d)
        return rcopy(ref, ref, ss2.at[it, m2], rs2.at[it, m2], chip(flip(grp, 1 << d), head), t)

    def over(it, mask):
        ref = part(it, mask, t)
        return rcopy(ref, ref, ss3.at[it, mask], rs3.at[it, mask], c, 1 - t)

    for it in range(8):
        hop(it, 0, 0).start()
    for it in range(8):
        over(it, 0).start()
    for r in range(3):
        dims = [order(it)[:r] for it in range(8)]
        for it in range(8):
            new = [m | (1 << order(it)[r]) for m in below(dims[it])]
            for m in new:
                got(part(it, m, t), rs2.at[it, m])
            if r < 2:
                for m in below(order(it)[:r + 1]):
                    hop(it, r + 1, m).start()
            for m in new:
                over(it, m).start()
    first_got((2, 3))
    for it in range(8):
        for m in range(8):
            got(part(it, m, 1 - t), rs3.at[it, m])
    for it in range(8):
        for r in range(3):
            for m in below(order(it)[:r]):
                hop(it, r, m).wait_send()
        for m in range(8):
            over(it, m).wait_send()
    first(sent, (0, 1, 2, 3))


def spread(q, do, k, v):
    dma = pltpu.SemaphoreType.DMA
    return pl.pallas_call(
        spread_kernel,
        out_shape=(shape((4 * UQ, G * HD), BF),) * 2 + (shape((S, HD), BF),) * 2, in_specs=[VM] * 4, out_specs=(VM,) * 4,
        scratch_shapes=[dma((4, 4, 2)), dma((4, 4, 2)), dma((8, 8)), dma((8, 8)), dma((8, 8)), dma((8, 8))],
        compiler_params=params(32, 2), name='spread')(q, do, k, v)


def gather_back_kernel(o_ref, dq_ref, dk_ref, dv_ref, ob_ref, dqb_ref, dkb_ref, dvb_ref, buf, rb, fin, ss1, rs1, ss2, rs2, ss3, rs3):
    c, t, grp, head = me()
    zb, yb, xb = head
    kb = (zb + yb) % 2
    hm = yb * 2 + xb
    greet(c, t, grp, head, True)

    def rows(it, mask, kk):
        return rd(unit_of(base_unit(flip(grp, mask), kk), it // 2) * UQ, UQ)

    def over(it, mask):
        return rcopy((dk_ref, dv_ref)[it % 2].at[rows(it, mask, 1 - t), :], buf.at[it, mask], ss2.at[it, mask], rs2.at[it, mask], c, 1 - t)

    def back(fn, kinds):
        for j in range(4):
            zs = (0, 1, 1, 0)[j]
            for e in range(2):
                par = e if j < 2 else 1 - e
                half = 0 if j < 2 else 1
                cc = quad_block(grp, t, zs, par)
                own = (cc == c) & (zb == t)
                for n in kinds:
                    wide = G * HD if n < 2 else HD
                    if n < 2:
                        src = (o_ref, dq_ref)[n].at[j * UQ + e * 128:j * UQ + (e + 1) * 128, :]
                    else:
                        src = fin.at[j * 2 + n - 2, e * 128:(e + 1) * 128, :]
                    dst = (ob_ref, dqb_ref, dkb_ref, dvb_ref)[n].at[half * 128:(half + 1) * 128, pl.ds(pl.multiple_of(hm * wide, wide), wide)]
                    fn(src, dst, ss1.at[j, e, n], rs1.at[hm, half, n], cc, zb, own)

    def back_got(kinds):
        for hh in range(4):
            for half in range(2):
                for n in kinds:
                    wide = G * HD if n < 2 else HD
                    dst = (ob_ref, dqb_ref, dkb_ref, dvb_ref)[n].at[half * 128:(half + 1) * 128, hh * wide:(hh + 1) * wide]
                    got(dst, rs1.at[hh, half, n])

    def hop(it, r, mask):
        d = order(it)[r]
        m2 = mask ^ (1 << d)
        return rcopy(buf.at[it, mask], rb.at[it, mask], ss3.at[it, mask], rs3.at[it, mask], chip(flip(grp, 1 << d), head), t), m2

    for r in (2, 1, 0):
        for it in range(8):
            for m in below(order(it)[:r]):
                over(it, m | (1 << order(it)[r])).start()
    for it in range(8):
        over(it, 0).start()
    back(send, (0, 1))
    for r in (2, 1, 0):
        for it in range(8):
            for m in [m | (1 << order(it)[r]) for m in below(order(it)[:r])]:
                got(buf.at[it, m], rs2.at[it, m])
                tot = buf[it, m] + (dk_ref, dv_ref)[it % 2][rows(it, m, t), :]
                for r2 in range(2, r, -1):
                    m3 = m | (1 << order(it)[r2])
                    got(rb.at[it, m3], rs3.at[it, m3])
                    tot = tot + rb[it, m3]
                buf[it, m] = tot
                hop(it, r, m)[0].start()
    for it in range(8):
        got(buf.at[it, 0], rs2.at[it, 0])
        tot = buf[it, 0] + (dk_ref, dv_ref)[it % 2][rows(it, 0, t), :]
        for r2 in range(3):
            m3 = 1 << order(it)[r2]
            got(rb.at[it, m3], rs3.at[it, m3])
            tot = tot + rb[it, m3]
        fin[it] = tot.astype(BF)
    back(send, (2, 3))
    for it in range(8):
        for m in range(8):
            over(it, m).wait_send()
            if m:
                r = max(order(it).index(d) for d in range(3) if (m >> d) & 1)
                hop(it, r, m)[0].wait_send()
    back_got((0, 1, 2, 3))
    back(sent, (0, 1, 2, 3))


def gather_back(o, dq, dk, dv):
    dma = pltpu.SemaphoreType.DMA
    return pl.pallas_call(
        gather_back_kernel,
        out_shape=(shape((256, 4 * G * HD), BF),) * 2 + (shape((256, 4 * HD), BF),) * 2, in_specs=[VM] * 4, out_specs=(VM,) * 4,
        scratch_shapes=[pltpu.VMEM((8, 8, UQ, HD), F32), pltpu.VMEM((8, 8, UQ, HD), F32), pltpu.VMEM((8, UQ, HD), BF),
                        dma((4, 2, 4)), dma((4, 2, 4)), dma((8, 8)), dma((8, 8)), dma((8, 8)), dma((8, 8))],
        compiler_params=params(56, 3), name='gather_back')(o, dq, dk, dv)


def fwd_body(i, q_ref, k_ref, v_ref, o_ref, l2_ref, sa, sb, p_scr, m_scr, ot_scr):
    NT = S // KT
    diff = (lax.broadcasted_iota(jnp.int32, (KT, UQ), 0) - lax.broadcasted_iota(jnp.int32, (KT, UQ), 1))

    def one(idx, _):
        j, h = idx // G, idx % G
        u = unit_of(i, j)
        nt = (u + 2) // 2
        qh = q_ref[pl.ds(pl.multiple_of(j * UQ, UQ), UQ), pl.ds(pl.multiple_of(h * HD, HD), HD)]

        def score(t):
            return dg(k_ref[pl.ds(pl.multiple_of(t * KT, KT), KT), :], qh, 1, 1)

        def soft(s_ref, t, m, l, masked):
            s = s_ref[...] * C2
            if masked:
                s = jnp.where(diff <= u * UQ - t * KT, s, NINF)
            s3 = s.reshape(KT // 8, 8, UQ)
            mn = jnp.maximum(m, jnp.max(s3, axis=0))
            p3 = jnp.exp2(s3 - mn[None])
            l = l * jnp.exp2(m - mn) + jnp.sum(p3, axis=0)
            p_scr[pl.ds(pl.multiple_of(t * KT, KT), KT), :] = p3.reshape(KT, UQ)
            m_scr[t] = mn
            return mn, l

        sa[...] = score(0)
        m0 = jnp.full((8, UQ), NEG, F32)
        l0 = jnp.zeros((8, UQ), F32)
        nf = nt - 1

        def pair(tt, c):
            m, l = c
            t = tt * 2
            sb[...] = score(t + 1)
            m, l = soft(sa, t, m, l, False)
            sa[...] = score(t + 2)
            m, l = soft(sb, t + 1, m, l, False)
            return m, l
        m, l = lax.fori_loop(0, nf // 2, pair, (m0, l0))

        def odd(c):
            m, l = c
            sb[...] = score(nf)
            m, l = soft(sa, nf - 1, m, l, False)
            m, l = soft(sb, nf, m, l, True)
            return m, l

        def even(c):
            m, l = c
            return soft(sa, nf, m, l, True)
        m, l = lax.cond(nf % 2 == 1, odd, even, (m, l))
        mt = jnp.max(m, axis=0, keepdims=True)
        lt = jnp.sum(l * jnp.exp2(m - mt), axis=0, keepdims=True)
        l2 = mt + jnp.log2(lt)
        l2_ref[pl.ds(idx, 1), :] = l2

        @pl.when(nt < NT)
        def _():
            p_scr[pl.ds(pl.multiple_of(nt * KT, KT), KT), :] = jnp.zeros((KT, UQ), F32)
            m_scr[nt] = jnp.full((8, UQ), NEG, F32)
        ot_scr[...] = jnp.zeros_like(ot_scr)

        def pv(tt, _):
            acc = None
            for e in range(2):
                t = tt * 2 + e
                f = jnp.exp2(m_scr[t] - l2)
                p = p_scr[pl.ds(pl.multiple_of(t * KT, KT), KT), :].reshape(KT // 8, 8, UQ)
                pb = (p * f[None]).reshape(KT, UQ).astype(BF)
                r = dg(v_ref[pl.ds(pl.multiple_of(t * KT, KT), KT), :], pb, 0, 0)
                acc = r if acc is None else acc + r
            ot_scr[...] += acc
            return 0
        lax.fori_loop(0, (nt + 1) // 2, pv, 0)
        o_ref[pl.ds(pl.multiple_of(j * UQ, UQ), UQ), pl.ds(pl.multiple_of(h * HD, HD), HD)] = ot_scr[...].T.astype(BF)
        return 0
    lax.fori_loop(0, 4 * G, one, 0)


def bwd_body(i, q_ref, do_ref, o_ref, l2_ref, k_ref, v_ref, dq_ref, dk_ref, dv_ref, d_scr, dqt_scr, dka, dva):
    NT = S // KT
    diff = (lax.broadcasted_iota(jnp.int32, (KT, UQ), 0) - lax.broadcasted_iota(jnp.int32, (KT, UQ), 1))

    def prep(idx, _):
        j, h = idx // G, idx % G
        rows = pl.ds(pl.multiple_of(j * UQ, UQ), UQ)
        cols = pl.ds(pl.multiple_of(h * HD, HD), HD)
        prod = do_ref[rows, cols].astype(F32) * o_ref[rows, cols].astype(F32)
        d_scr[pl.ds(idx, 1), :] = jnp.sum(prod.T, axis=0, keepdims=True)
        dqt_scr[idx] = jnp.zeros((HD, UQ), F32)
        return 0
    lax.fori_loop(0, 4 * G, prep, 0)

    def tile(tt, _):
        t = NT - 1 - tt
        krows = pl.ds(pl.multiple_of(t * KT, KT), KT)
        dka[...] = jnp.zeros_like(dka)
        dva[...] = jnp.zeros_like(dva)

        def step(j, masked):
            u = unit_of(i, j)
            rows = pl.ds(pl.multiple_of(j * UQ, UQ), UQ)
            k = k_ref[krows, :]
            v = v_ref[krows, :]
            dv = None
            dk = None
            for h in range(G):
                idx = j * G + h
                cols = slice(h * HD, (h + 1) * HD)
                q = q_ref[rows, cols]
                do = do_ref[rows, cols]
                s = dg(k, q, 1, 1) * C2
                if masked:
                    s = jnp.where(diff <= u * UQ - t * KT, s, NINF)
                pb = jnp.exp2(s - l2_ref[pl.ds(idx, 1), :]).astype(BF)
                dp = dg(v, do, 1, 1)
                ds = (pb.astype(F32) * (dp - d_scr[pl.ds(idx, 1), :])).astype(BF)
                r1 = dg(pb, do, 1, 0)
                r2 = dg(ds, q, 1, 0)
                dv = r1 if dv is None else dv + r1
                dk = r2 if dk is None else dk + r2
                dqt_scr[idx] += dg(k, ds, 0, 0)
            dva[...] += dv
            dka[...] += dk

        for jj in range(4):
            j = 3 - jj
            u = unit_of(i, j)
            @pl.when(u // 2 > t)
            def _():
                step(j, False)

            @pl.when(u // 2 == t)
            def _():
                step(j, True)
        dk_ref[krows, :] = dka[...] * TSC
        dv_ref[krows, :] = dva[...]
        return 0
    lax.fori_loop(0, NT, tile, 0)

    def fin(idx, _):
        j, h = idx // G, idx % G
        rows = pl.ds(pl.multiple_of(j * UQ, UQ), UQ)
        cols = pl.ds(pl.multiple_of(h * HD, HD), HD)
        dq_ref[rows, cols] = (dqt_scr[idx] * TSC).T.astype(BF)
        return 0
    lax.fori_loop(0, 4 * G, fin, 0)


def fwd_kernel(*refs):
    _, t, grp, _ = me()
    fwd_body(base_unit(grp, t), *refs)


def bwd_kernel(*refs):
    _, t, grp, _ = me()
    bwd_body(base_unit(grp, t), *refs)


def attention_fwd(q, k, v):
    return pl.pallas_call(
        fwd_kernel, out_shape=(shape((4 * UQ, G * HD), BF), shape((4 * G, UQ), F32)), in_specs=[VM] * 3, out_specs=(VM, VM),
        scratch_shapes=[pltpu.VMEM((KT, UQ), F32), pltpu.VMEM((KT, UQ), F32), pltpu.VMEM((S, UQ), F32),
                        pltpu.VMEM((S // KT, 8, UQ), F32), pltpu.VMEM((HD, UQ), F32)],
        compiler_params=params(60), name='attention_fwd')(q, k, v)


def attention_bwd(q, do, o, l2, k, v):
    return pl.pallas_call(
        bwd_kernel, out_shape=(shape((4 * UQ, G * HD), BF), shape((S, HD), F32), shape((S, HD), F32)), in_specs=[VM] * 6, out_specs=(VM,) * 3,
        scratch_shapes=[pltpu.VMEM((4 * G, UQ), F32), pltpu.VMEM((4 * G, HD, UQ), F32), pltpu.VMEM((KT, HD), F32), pltpu.VMEM((KT, HD), F32)],
        compiler_params=params(60), name='attention_bwd')(q, do, o, l2, k, v)


def solution(mesh):
    row_spec = P(('dp', 'cp', 'tp'), None)

    def local_step(x_blk, dy_blk, w_query, w_key, w_value, w_out):
        x_loc, dy_loc = pair_gather(x_blk, dy_blk)
        keys = dg(x_loc, w_key, 1, 0).astype(BF)
        values = dg(x_loc, w_value, 1, 0).astype(BF)
        query = dg(x_loc, w_query, 1, 0).astype(BF)
        d_out = dg(dy_loc, w_out, 1, 1).astype(BF)
        q, do, k, v = spread(query, d_out, keys, values)
        o, l2 = attention_fwd(q, k, v)
        dq, dk, dv = attention_bwd(q, do, o, l2, k, v)
        ob, dqb, dkb, dvb = gather_back(o, dq, dk, dv)
        y_part = dg(ob, w_out, 1, 0)
        dx_part = dg(dqb, w_query, 1, 1) + dg(dkb, w_key, 1, 1) + dg(dvb, w_value, 1, 1)
        y_in, dx_in = pair_half(y_part, dx_part)
        n = y_in.shape[0]
        start = lax.axis_index('tp') * n
        y_own = lax.dynamic_slice_in_dim(y_part, start, n, 0)
        dx_own = lax.dynamic_slice_in_dim(dx_part, start, n, 0)
        return (y_own + y_in).astype(BF), (dx_own + dx_in).astype(BF)

    return jax.shard_map(local_step, mesh=mesh, in_specs=(row_spec, row_spec, P(None, 'tp'), P(None, 'tp'), P(None, 'tp'), P('tp', None)), out_specs=(row_spec, row_spec), check_vma=False)
```

time: 3000 us -> 395 us (0.13)
  matrix products: 1590 us -> 21.5 us
  waiting for transfers between devices: 1100 us -> 0 us
  Pallas kernels: 0 us -> 357 us
  other arithmetic: 256 us -> 4.36 us
    dot_general x104 -> x8, matrix products: 1590 us -> 21.5 us  [dg(): lax.dot_general(a, b, (((ca,), (cb,)), ((), ())), preferred_element_type=...]
    reduce_scatter x4 -> x0, waiting for transfers between devices: 886 us -> none  [the longest x1 448 us: local_step(): lax.psum_scatter(dv_part, 'cp', scatter_dimension=0, tiled=True)]
    pallas_call x0 -> x6, Pallas kernels: none -> 357 us  [the longest x1 102 us: gather_back(): pl.pallas_call(gather_back_kernel, out_shape=(shape((256, 4 * G * HD), BF...]
    all_gather x4 -> x0, waiting for transfers between devices: 213 us -> none  [the longest x1 107 us: local_step(): keys_all = lax.all_gather(keys_loc, 'cp', axis=0, tiled=True)]
    convert_element_type x20 -> x1, other arithmetic: 149 us -> 4.36 us  [local_step(): return ((y_own + y_in).astype(BF), (dx_own + dx_in).astype(BF))]
    reduce_sum x16 -> x0, other arithmetic: 102 us -> none  [block_step(): log_norm = jax.nn.logsumexp(scores, axis=-1, keepdims=True)]
  transfers between devices with their start and end apart: 8 -> 0, of which waited for: 8 -> 0; matrix products, arithmetic and copies ran while one was open for 2% -> 0% of each run, Pallas kernels for 0% -> 0%
where the time goes in v1:
time: 395 us
  Pallas kernels  357 us (90%)
  matrix products  21.5 us (5%)
  local copies, waits for them, and re-layouts  11.4 us (3%)
  other arithmetic  4.36 us (1%)
    pallas_call x1, Pallas kernels, gather_back(): pl.pallas_call(gather_back_kernel, out_shape=(shape((256, 4 * G * HD), BF...  102 us
    pallas_call x1, Pallas kernels, attention_bwd(): pl.pallas_call(bwd_kernel, out_shape=(shape((4 * UQ, G * HD), BF), shape(...  99.2 us
    pallas_call x1, Pallas kernels, attention_fwd(): pl.pallas_call(fwd_kernel, out_shape=(shape((4 * UQ, G * HD), BF), shape(...  78.5 us
    pallas_call x1, Pallas kernels, spread(): pl.pallas_call(spread_kernel, out_shape=(shape((4 * UQ, G * HD), BF),) *...  67 us
    dot_general x8, matrix products, dg(): lax.dot_general(a, b, (((ca,), (cb,)), ((), ())), preferred_element_type=...  21.5 us
    unnamed x44, local copies, waits for them, and re-layouts  11.4 us

profile of v1, /device:TPU:1, one launch (start us, length us, event | category | flops | bytes accessed | tf_op | source)
XLA Modules:
  0.0 395.0 jit_solution(18221564155745015789)
XLA Ops:
  0.6 0.0 copy-start
  0.6 0.0 copy-start.8
  0.7 1.3 copy-done.8
  1.9 1.1 copy-done.9
  3.1 4.4 %pair_gather.1 = (bf16[256,3072]{1,0:T(8,128)(2,1)S(1)}, bf16[256,3072]{1,0:T(8,128)(2,1)S(1)}) custom-call(bf16[128,3072]{1,0:T(8,128)(2,1)S(1)} %copy-done.8, bf16[128,3072]{1,0:T(8,128)(2,1)S(1)} %copy-done.9), custom_call_target="tpu_custom_call" | custom-call | tf_op jit(solution)/shard_map/pair_gather/pallas_call | solution.py:161
  7.5 0.0 copy-start.11
  7.5 0.0 slice-start.1
  7.5 0.0 slice-start.2
  7.5 6.4 %convolution_convert_fusion.1.q_ref = bf16[256,1536]{1,0:T(8,128)(2,1)S(1)} fusion(bf16[256,3072]{1,0:T(8,128)(2,1)S(1)} %get-tuple-element.19, bf16[3072,1536]{1,0:T(8,128)(2,1)} %param.8), kind=kOutput, calls=%fused_computation.3 | convolution fusion | flops 2416312320 | bytes 11796480 | tf_op jit(solution)/shard_map/dot_general | solution.py:25
  14.0 0.0 copy-done.11
  14.0 1.0 convolution_convert_fusion.2.v_ref
  15.0 0.0 copy-done
  15.0 1.0 convolution_convert_fusion.3.k_ref
  15.9 0.0 slice-done
  16.0 0.0 slice-done.1
  16.0 0.0 slice-done.2
  16.0 2.6 convolution_convert_fusion.do_ref
  18.6 67.0 %spread.1 = (bf16[1024,384]{1,0:T(8,128)(2,1)S(1)}, bf16[1024,384]{1,0:T(8,128)(2,1)S(1)}, bf16[16384,128]{1,0:T(8,128)(2,1)S(1)}, bf16[16384,128]{1,0:T(8,128)(2,1)S(1)}) custom-call(bf16[256,1536]{1,0:T(8,128)(2,1)S(1)} %convolution_convert_fusion.1.q_ref, bf16[256,1536]{1,0:T(8,128)(2,1)S(1)} %convolution_convert_fusion.do_ref, ...), custom_call_target="tpu_custom_call" | custom-call | tf_op jit(solution)/shard_map/spread/pallas_call | solution.py:272
  85.6 0.0 copy-start.2
  85.6 1.9 copy-done.2
  87.6 2.0 copy-done.3
  89.6 0.9 copy-done.5
  90.5 0.9 copy-done.10
  91.3 78.5 %attention_fwd.1 = (bf16[1024,384]{1,0:T(8,128)(2,1)}, f32[12,256]{1,0:T(8,128)}) custom-call(bf16[1024,384]{1,0:T(8,128)(2,1)} %copy-done.5, bf16[16384,128]{1,0:T(8,128)(2,1)} %copy-done.2, bf16[16384,128]{1,0:T(8,128)(2,1)} %copy-done.3), custom_call_target="tpu_custom_call" | custom-call | tf_op jit(solution)/shard_map/attention_fwd/pallas_call | solution.py:529
  169.9 99.2 %attention_bwd.1 = (bf16[1024,384]{1,0:T(8,128)(2,1)}, f32[16384,128]{1,0:T(8,128)}, f32[16384,128]{1,0:T(8,128)}) custom-call(bf16[1024,384]{1,0:T(8,128)(2,1)} %copy-done.5, bf16[1024,384]{1,0:T(8,128)(2,1)} %copy-done.10, bf16[1024,384]{1,0:T(8,128)(2,1)} %get-tuple-element.24.refs_2_.o_ref, f32[12,256]{1,0:T(8,128)} %get-tuple-element.26.refs_3_, ...), custom_call_target="tpu_custom_call" | custom-call | tf_op jit(solution)/shard_map/attention_bwd/pallas_call | solution.py:537
  269.1 101.8 %gather_back.1 = (bf16[256,1536]{1,0:T(8,128)(2,1)}, bf16[256,1536]{1,0:T(8,128)(2,1)}, bf16[256,512]{1,0:T(8,128)(2,1)}, bf16[256,512]{1,0:T(8,128)(2,1)}) custom-call(bf16[1024,384]{1,0:T(8,128)(2,1)} %get-tuple-element.24.refs_2_.o_ref, bf16[1024,384]{1,0:T(8,128)(2,1)} %get-tuple-element.27.dq_ref, f32[16384,128]{1,0:T(8,128)} %get-tuple-element.28.dk_ref, ...), custom_call_target="tpu_custom_call" | custom-call | tf_op jit(solution)/shard_map/gather_back/pallas_call | solution.py:361
  370.9 0.0 copy-start.14
  370.9 0.0 slice-start.3
  370.9 0.0 slice-start.4
  371.0 5.6 %fusion.1 = f32[256,3072]{1,0:T(8,128)S(1)} fusion(bf16[256,1536]{1,0:T(8,128)(2,1)} %get-tuple-element.31, bf16[3072,1536]{1,0:T(8,128)(2,1)} %param.8), kind=kOutput, calls=%fused_computation.9 | convolution fusion | flops 2415919104 | bytes 13369344 | tf_op jit(solution)/shard_map/dot_general | solution.py:25
  376.5 0.0 copy-done.14
  376.6 0.0 copy-start.12
  376.6 0.0 copy-start.13
  376.6 0.0 slice-start.5
  376.6 1.1 convolution_add_fusion.1
  377.7 0.7 copy-done.12
  378.4 0.0 copy-done.13
  378.5 1.0 convolution_add_fusion.dx_ref
  379.5 0.0 copy-start.1
  379.5 0.0 slice-done.3
  379.5 0.0 slice-done.4
  379.5 0.0 slice-done.5
  379.5 0.1 copy-done.15
  379.7 2.8 fusion.y_ref
  382.5 5.8 %pair_half.1 = (f32[128,3072]{1,0:T(8,128)S(1)}, f32[128,3072]{1,0:T(8,128)S(1)}) custom-call(f32[256,3072]{1,0:T(8,128)S(1)} %fusion.y_ref, f32[256,3072]{1,0:T(8,128)S(1)} %convolution_add_fusion.dx_ref), custom_call_target="tpu_custom_call" | custom-call | tf_op jit(solution)/shard_map/pair_half/pallas_call | solution.py:183
  388.3 1.2 copy-done.6
  389.5 1.1 copy-done.7
  390.6 4.4 %add_convert_fusion = (bf16[128,3072]{1,0:T(8,128)(2,1)}, bf16[128,3072]{1,0:T(8,128)(2,1)}) fusion(f32[128,3072]{1,0:T(8,128)} %copy-done.7, f32[256,3072]{1,0:T(8,128)} %copy-done.1, s32[]{:T(128)S(6)} %select_n.4, f32[128,3072]{1,0:T(8,128)} %copy-done.6, f32[256,3072]{1,0:T(8,128)} %copy-done.4), kind=kLoop, calls=%fused_computation.4 | loop fusion | flops 1572864 | bytes 7864324 | tf_op jit(solution)/shard_map/convert_element_type | solution.py:563
  (13 shorter events, 0.0 us)
Async XLA Ops:
  0.6 14.3 %copy-start = (bf16[3072,512]{1,0:T(8,128)(2,1)S(1)}, bf16[3072,512]{1,0:T(8,128)(2,1)}, u32[]{:S(2)}) copy-start(bf16[3072,512]{1,0:T(8,128)(2,1)} %param.9) | copy-start | bytes 9437188
  0.6 1.3 copy-start.8
  1.9 1.1 copy-start.9
  3.1 12.9 %slice-start = ((s8[9437184]{0:T(1024)(128)(4,1)}), s8[4194304]{0:T(1024)(128)(4,1)S(1)}, s32[]{:S(2)}) async-start(s8[9437184]{0:T(1024)(128)(4,1)} %bitcast.16), calls=%async_computation | async-start | bytes 8388608
  7.5 6.5 %copy-start.11 = (bf16[3072,512]{1,0:T(8,128)(2,1)S(1)}, bf16[3072,512]{1,0:T(8,128)(2,1)}, u32[]{:S(2)}) copy-start(bf16[3072,512]{1,0:T(8,128)(2,1)} %param.10) | copy-start | bytes 9437188
  7.5 8.4 %slice-start.1 = ((s8[9437184]{0:T(1024)(128)(4,1)}), s8[4194304]{0:T(1024)(128)(4,1)S(1)}, s32[]{:S(2)}) async-start(s8[9437184]{0:T(1024)(128)(4,1)} %bitcast.16), calls=%async_computation.1 | async-start | bytes 8388608
  7.5 8.4 %slice-start.2 = ((s8[9437184]{0:T(1024)(128)(4,1)}), s8[1048576]{0:T(1024)(128)(4,1)S(1)}, s32[]{:S(2)}) async-start(s8[9437184]{0:T(1024)(128)(4,1)} %bitcast.16), calls=%async_computation.2 | async-start | bytes 2097152
  85.6 2.0 copy-start.2
  87.6 2.0 copy-start.3
  89.6 0.9 copy-start.5
  90.5 0.9 copy-start.10
  370.9 5.6 %copy-start.14 = (bf16[256,512]{1,0:T(8,128)(2,1)S(1)}, bf16[256,512]{1,0:T(8,128)(2,1)}, u32[]{:S(2)}) copy-start(bf16[256,512]{1,0:T(8,128)(2,1)} %get-tuple-element.32) | copy-start | bytes 786436
  370.9 8.6 %slice-start.3 = ((s8[9437184]{0:T(1024)(128)(4,1)}), s8[4194304]{0:T(1024)(128)(4,1)S(1)}, s32[]{:S(2)}) async-start(s8[9437184]{0:T(1024)(128)(4,1)} %bitcast.18), calls=%async_computation.3 | async-start | bytes 8388608
  370.9 8.6 %slice-start.4 = ((s8[9437184]{0:T(1024)(128)(4,1)}), s8[4194304]{0:T(1024)(128)(4,1)S(1)}, s32[]{:S(2)}) async-start(s8[9437184]{0:T(1024)(128)(4,1)} %bitcast.18), calls=%async_computation.4 | async-start | bytes 8388608
  376.6 1.9 copy-start.12
  376.6 1.9 copy-start.13
  376.6 2.9 slice-start.5
  378.5 1.2 copy-start.15
  379.5 3.0 copy-start.1
  382.4 5.8 %copy-start.4 = (f32[256,3072]{1,0:T(8,128)}, f32[256,3072]{1,0:T(8,128)S(1)}, u32[]{:S(2)}) copy-start(f32[256,3072]{1,0:T(8,128)S(1)} %fusion.y_ref) | copy-start | bytes 9437188
  388.3 1.2 copy-start.6
  389.5 1.1 copy-start.7

commit v2 on v1

--- a/solution.py
+++ b/solution.py
@@ -11,7 +11,11 @@
 S = 16384
 G = 3
 KT = 512
+CH = 128
+NG = 4
+TG = KT * NG
 UQ = 256
+LAGS = (3, 7, 11, 15)
 C2 = (HD ** -0.5) * 1.4426950408889634
 TSC = HD ** -0.5
 NEG = float(jnp.finfo(jnp.float32).min)
@@ -276,200 +280,250 @@
         compiler_params=params(32, 2), name='spread')(q, do, k, v)
 
 
-def gather_back_kernel(o_ref, dq_ref, dk_ref, dv_ref, ob_ref, dqb_ref, dkb_ref, dvb_ref, buf, rb, fin, ss1, rs1, ss2, rs2, ss3, rs3):
-    c, t, grp, head = me()
-    zb, yb, xb = head
-    kb = (zb + yb) % 2
-    hm = yb * 2 + xb
-    greet(c, t, grp, head, True)
-
-    def rows(it, mask, kk):
-        return rd(unit_of(base_unit(flip(grp, mask), kk), it // 2) * UQ, UQ)
-
-    def over(it, mask):
-        return rcopy((dk_ref, dv_ref)[it % 2].at[rows(it, mask, 1 - t), :], buf.at[it, mask], ss2.at[it, mask], rs2.at[it, mask], c, 1 - t)
-
-    def back(fn, kinds):
-        for j in range(4):
-            zs = (0, 1, 1, 0)[j]
-            for e in range(2):
-                par = e if j < 2 else 1 - e
-                half = 0 if j < 2 else 1
-                cc = quad_block(grp, t, zs, par)
-                own = (cc == c) & (zb == t)
-                for n in kinds:
-                    wide = G * HD if n < 2 else HD
-                    if n < 2:
-                        src = (o_ref, dq_ref)[n].at[j * UQ + e * 128:j * UQ + (e + 1) * 128, :]
-                    else:
-                        src = fin.at[j * 2 + n - 2, e * 128:(e + 1) * 128, :]
-                    dst = (ob_ref, dqb_ref, dkb_ref, dvb_ref)[n].at[half * 128:(half + 1) * 128, pl.ds(pl.multiple_of(hm * wide, wide), wide)]
-                    fn(src, dst, ss1.at[j, e, n], rs1.at[hm, half, n], cc, zb, own)
-
-    def back_got(kinds):
-        for hh in range(4):
-            for half in range(2):
-                for n in kinds:
-                    wide = G * HD if n < 2 else HD
-                    dst = (ob_ref, dqb_ref, dkb_ref, dvb_ref)[n].at[half * 128:(half + 1) * 128, hh * wide:(hh + 1) * wide]
-                    got(dst, rs1.at[hh, half, n])
-
-    def hop(it, r, mask):
-        d = order(it)[r]
-        m2 = mask ^ (1 << d)
-        return rcopy(buf.at[it, mask], rb.at[it, mask], ss3.at[it, mask], rs3.at[it, mask], chip(flip(grp, 1 << d), head), t), m2
-
-    for r in (2, 1, 0):
-        for it in range(8):
-            for m in below(order(it)[:r]):
-                over(it, m | (1 << order(it)[r])).start()
-    for it in range(8):
-        over(it, 0).start()
-    back(send, (0, 1))
-    for r in (2, 1, 0):
-        for it in range(8):
-            for m in [m | (1 << order(it)[r]) for m in below(order(it)[:r])]:
-                got(buf.at[it, m], rs2.at[it, m])
-                tot = buf[it, m] + (dk_ref, dv_ref)[it % 2][rows(it, m, t), :]
-                for r2 in range(2, r, -1):
-                    m3 = m | (1 << order(it)[r2])
-                    got(rb.at[it, m3], rs3.at[it, m3])
-                    tot = tot + rb[it, m3]
-                buf[it, m] = tot
-                hop(it, r, m)[0].start()
-    for it in range(8):
-        got(buf.at[it, 0], rs2.at[it, 0])
-        tot = buf[it, 0] + (dk_ref, dv_ref)[it % 2][rows(it, 0, t), :]
-        for r2 in range(3):
-            m3 = 1 << order(it)[r2]
-            got(rb.at[it, m3], rs3.at[it, m3])
-            tot = tot + rb[it, m3]
-        fin[it] = tot.astype(BF)
-    back(send, (2, 3))
-    for it in range(8):
-        for m in range(8):
-            over(it, m).wait_send()
-            if m:
-                r = max(order(it).index(d) for d in range(3) if (m >> d) & 1)
-                hop(it, r, m)[0].wait_send()
-    back_got((0, 1, 2, 3))
-    back(sent, (0, 1, 2, 3))
-
-
-def gather_back(o, dq, dk, dv):
-    dma = pltpu.SemaphoreType.DMA
-    return pl.pallas_call(
-        gather_back_kernel,
-        out_shape=(shape((256, 4 * G * HD), BF),) * 2 + (shape((256, 4 * HD), BF),) * 2, in_specs=[VM] * 4, out_specs=(VM,) * 4,
-        scratch_shapes=[pltpu.VMEM((8, 8, UQ, HD), F32), pltpu.VMEM((8, 8, UQ, HD), F32), pltpu.VMEM((8, UQ, HD), BF),
-                        dma((4, 2, 4)), dma((4, 2, 4)), dma((8, 8)), dma((8, 8)), dma((8, 8)), dma((8, 8))],
-        compiler_params=params(56, 3), name='gather_back')(o, dq, dk, dv)
-
-
-def fwd_body(i, q_ref, k_ref, v_ref, o_ref, l2_ref, sa, sb, p_scr, m_scr, ot_scr):
-    NT = S // KT
-    diff = (lax.broadcasted_iota(jnp.int32, (KT, UQ), 0) - lax.broadcasted_iota(jnp.int32, (KT, UQ), 1))
+def transpose_into(x_ref, xt_ref, n):
+    def body(t, _):
+        r = pl.ds(pl.multiple_of(t * KT, KT), KT)
+        xt_ref[:, r] = x_ref[r, :].T
+        return 0
+    lax.fori_loop(0, n // KT, body, 0)
+
+
+def rows_of(j):
+    return pl.ds(pl.multiple_of(j * UQ, UQ), UQ)
+
+
+def cols_of(h):
+    return pl.ds(pl.multiple_of(h * HD, HD), HD)
+
+
+def fwd_body(i, q_ref, k_ref, v_ref, o_ref, l2_ref, sa, sb, p_scr, m_scr, ot_scr, vt_scr, qt_scr):
+    diff = (lax.broadcasted_iota(jnp.int32, (CH, UQ), 0) - lax.broadcasted_iota(jnp.int32, (CH, UQ), 1))
+    transpose_into(v_ref, vt_scr, S)
+    NC = KT // CH
 
     def one(idx, _):
         j, h = idx // G, idx % G
         u = unit_of(i, j)
-        nt = (u + 2) // 2
-        qh = q_ref[pl.ds(pl.multiple_of(j * UQ, UQ), UQ), pl.ds(pl.multiple_of(h * HD, HD), HD)]
+        ng = (u * UQ) // TG + 1
+        qt_scr[...] = q_ref[rows_of(j), cols_of(h)].T
 
         def score(t):
-            return dg(k_ref[pl.ds(pl.multiple_of(t * KT, KT), KT), :], qh, 1, 1)
+            return dg(k_ref[pl.ds(pl.multiple_of(t * KT, KT), KT), :], qt_scr[...], 1, 0)
 
         def soft(s_ref, t, m, l, masked):
-            s = s_ref[...] * C2
-            if masked:
-                s = jnp.where(diff <= u * UQ - t * KT, s, NINF)
-            s3 = s.reshape(KT // 8, 8, UQ)
-            mn = jnp.maximum(m, jnp.max(s3, axis=0))
-            p3 = jnp.exp2(s3 - mn[None])
-            l = l * jnp.exp2(m - mn) + jnp.sum(p3, axis=0)
-            p_scr[pl.ds(pl.multiple_of(t * KT, KT), KT), :] = p3.reshape(KT, UQ)
-            m_scr[t] = mn
-            return mn, l
+            for c in range(NC):
+                s = s_ref[c * CH:(c + 1) * CH, :] * C2
+                if masked:
+                    s = jnp.where(diff <= u * UQ - t * KT - c * CH, s, NINF)
+                s3 = s.reshape(CH // 8, 8, UQ)
+                mn = jnp.maximum(m, jnp.max(s3, axis=0))
+                p3 = jnp.exp2(s3 - mn[None])
+                l = l * jnp.exp2(m - mn) + jnp.sum(p3, axis=0)
+                m = mn
+                p_scr[pl.ds(pl.multiple_of(t * KT + c * CH, CH), CH), :] = p3.reshape(CH, UQ)
+                m_scr[t * NC + c] = mn
+            return m, l
 
         sa[...] = score(0)
         m0 = jnp.full((8, UQ), NEG, F32)
         l0 = jnp.zeros((8, UQ), F32)
-        nf = nt - 1
-
-        def pair(tt, c):
+
+        def group(g, c, masked):
             m, l = c
-            t = tt * 2
-            sb[...] = score(t + 1)
-            m, l = soft(sa, t, m, l, False)
-            sa[...] = score(t + 2)
-            m, l = soft(sb, t + 1, m, l, False)
+            t = g * NG
+            for e in range(1, NG):
+                sb[e - 1] = score(t + e)
+            m, l = soft(sa, t, m, l, masked)
+            if not masked:
+                sa[...] = score(t + NG)
+            for e in range(1, NG):
+                m, l = soft(sb.at[e - 1], t + e, m, l, masked)
             return m, l
-        m, l = lax.fori_loop(0, nf // 2, pair, (m0, l0))
-
-        def odd(c):
-            m, l = c
-            sb[...] = score(nf)
-            m, l = soft(sa, nf - 1, m, l, False)
-            m, l = soft(sb, nf, m, l, True)
-            return m, l
-
-        def even(c):
-            m, l = c
-            return soft(sa, nf, m, l, True)
-        m, l = lax.cond(nf % 2 == 1, odd, even, (m, l))
+        m, l = lax.fori_loop(0, ng - 1, lambda g, c: group(g, c, False), (m0, l0))
+        m, l = group(ng - 1, (m, l), True)
         mt = jnp.max(m, axis=0, keepdims=True)
         lt = jnp.sum(l * jnp.exp2(m - mt), axis=0, keepdims=True)
         l2 = mt + jnp.log2(lt)
         l2_ref[pl.ds(idx, 1), :] = l2
-
-        @pl.when(nt < NT)
-        def _():
-            p_scr[pl.ds(pl.multiple_of(nt * KT, KT), KT), :] = jnp.zeros((KT, UQ), F32)
-            m_scr[nt] = jnp.full((8, UQ), NEG, F32)
         ot_scr[...] = jnp.zeros_like(ot_scr)
 
-        def pv(tt, _):
+        def pv(g, _):
             acc = None
-            for e in range(2):
-                t = tt * 2 + e
-                f = jnp.exp2(m_scr[t] - l2)
-                p = p_scr[pl.ds(pl.multiple_of(t * KT, KT), KT), :].reshape(KT // 8, 8, UQ)
-                pb = (p * f[None]).reshape(KT, UQ).astype(BF)
-                r = dg(v_ref[pl.ds(pl.multiple_of(t * KT, KT), KT), :], pb, 0, 0)
+            for e in range(NG):
+                t = g * NG + e
+                ps = []
+                for c in range(NC):
+                    f = jnp.exp2(m_scr[t * NC + c] - l2)
+                    p = p_scr[pl.ds(pl.multiple_of(t * KT + c * CH, CH), CH), :].reshape(CH // 8, 8, UQ)
+                    ps.append((p * f[None]).reshape(CH, UQ).astype(BF))
+                r = dg(vt_scr[:, pl.ds(pl.multiple_of(t * KT, KT), KT)], jnp.concatenate(ps, 0), 1, 0)
                 acc = r if acc is None else acc + r
             ot_scr[...] += acc
             return 0
-        lax.fori_loop(0, (nt + 1) // 2, pv, 0)
-        o_ref[pl.ds(pl.multiple_of(j * UQ, UQ), UQ), pl.ds(pl.multiple_of(h * HD, HD), HD)] = ot_scr[...].T.astype(BF)
+        lax.fori_loop(0, ng, pv, 0)
+        o_ref[rows_of(j), cols_of(h)] = ot_scr[...].T.astype(BF)
         return 0
     lax.fori_loop(0, 4 * G, one, 0)
 
 
-def bwd_body(i, q_ref, do_ref, o_ref, l2_ref, k_ref, v_ref, dq_ref, dk_ref, dv_ref, d_scr, dqt_scr, dka, dva):
+def owners(t):
+    j = t // 8
+    odd, hi = j % 2, j // 2
+    h = (1 - 2 * odd) * t + odd * (15 + 16 * hi) - (1 - odd) * 16 * hi
+    za, yk = h // 4, h % 4
+    k = yk // 2
+    return j, k, za, yk + k * (3 - 2 * yk), (odd + k) % 2
+
+
+def bwd_kernel(q_ref, do_ref, o_ref, l2_ref, k_ref, v_ref, ob_ref, dqb_ref, dkb_ref, dvb_ref,
+               dq_ref, dkv, d_scr, dqt_scr, qt_scr, dot_scr, s_scr, dp_scr,
+               rb0, rb1, rb2, rb3, fin, ssb, rsb, ss0, rs0, ss1, rs1, ss2, rs2, ss3, rs3):
+    c, t_me, grp, head = me()
+    zb, yb, xb = head
+    hm = yb * 2 + xb
+    i = base_unit(grp, t_me)
     NT = S // KT
+    nbrs = [chip(flip(grp, 1 << d), head) for d in range(3)]
+
+    def back(fn, j, n):
+        zs = ((j + 1) // 2) % 2
+        half = j // 2
+        for e in range(2):
+            par = e + half * (1 - 2 * e)
+            cc = quad_block(grp, t_me, zs, par)
+            own = (cc == c) & (zb == t_me)
+            wide = G * HD if n < 2 else HD
+            if n < 2:
+                src = (o_ref, dq_ref)[n].at[rd(j * UQ + e * 128, 128), :]
+            else:
+                src = fin.at[j, n - 2, e * 128:(e + 1) * 128, :]
+            dst = (ob_ref, dqb_ref, dkb_ref, dvb_ref)[n].at[rd(half * 128, 128), pl.ds(pl.multiple_of(hm * wide, wide), wide)]
+            fn(src, dst, ssb.at[j, e, n], rsb.at[hm, half, n], cc, zb, own)
+
+    def back_got(n):
+        wide = G * HD if n < 2 else HD
+        for hh in range(4):
+            for half in range(2):
+                got((ob_ref, dqb_ref, dkb_ref, dvb_ref)[n].at[half * 128:(half + 1) * 128, hh * wide:(hh + 1) * wide], rsb.at[hh, half, n])
+
+    def item(n, e):
+        t = tile_at(n)
+        j, k, za, ya, s0 = owners(t)
+        hi = j // 2
+        same = [za == grp[0], ya == grp[1], (s0 + e) % 2 == grp[2]]
+        if e:
+            same = same[::-1]
+            slots = [(j * 2 + 1) * 4 + za * 2 + ya, hi * 4 + za * 2 + ya, hi * 2 + za, hi]
+        else:
+            slots = [j * 8 + za * 2 + ya, j * 2 + ya, j, hi]
+        there = [k == t_me]
+        for d in range(3):
+            there.append(there[d] & same[d])
+        sends = [k != t_me] + [there[d] & jnp.logical_not(same[d]) for d in range(3)]
+        return 2 * t + e, j, slots, there, sends
+
+    def link(n, e, u, slots, r):
+        if r == 0:
+            return rcopy(dkv.at[u], rb0.at[slots[0]], ss0.at[slots[0]], rs0.at[slots[0]], c, 1 - t_me)
+        rb, ss, rs = ((rb1, ss1, rs1), (rb2, ss2, rs2), (rb3, ss3, rs3))[r - 1]
+        return rcopy(rb0.at[slots[0]], rb.at[e, slots[r]], ss.at[e, slots[r]], rs.at[e, slots[r]], nbrs[3 - r if e else r - 1], t_me)
+
+    def over(n):
+        for e in range(2):
+            u, _, slots, _, sends = item(n, e)
+
+            @pl.when(sends[0])
+            def _():
+                link(n, e, u, slots, 0).start()
+
+    def stage(n, r):
+        for e in range(2):
+            u, j, slots, there, sends = item(n, e)
+            acc = rb0.at[slots[0]]
+
+            @pl.when(there[r])
+            def _():
+                if r == 0:
+                    got(acc, rs0.at[slots[0]])
+                    acc[...] = acc[...] + dkv[u]
+                else:
+                    rb, rs = ((rb1, rs1), (rb2, rs2), (rb3, rs3))[r - 1]
+                    new = rb.at[e, slots[r]]
+                    got(new, rs.at[e, slots[r]])
+                    if r < 3:
+                        acc[...] = acc[...] + new[...]
+                    else:
+                        fin[j, 0] = ((acc[0] + new[0]) * TSC).astype(BF)
+                        fin[j, 1] = (acc[1] + new[1]).astype(BF)
+                        back(send, j, 2)
+                        back(send, j, 3)
+            if r < 3:
+                @pl.when(sends[r + 1])
+                def _():
+                    link(n, e, u, slots, r + 1).start()
+
+    def tile_at(n):
+        n = jnp.minimum(n, NT - 1)
+        b, a, w = n // 8, (n // 2) % 4, n % 2
+        low = 4 * (b + 1 - 2 * (b % 2)) + a + 2 - 4 * (a // 2)
+        return (1 - w) * (31 - 4 * b - a) + w * low
+
+    def sums(n):
+        for r in range(4):
+            m = n - LAGS[r]
+
+            @pl.when((m >= 0) & (m < NT))
+            def _():
+                stage(m, r)
+
+    greet(c, t_me, grp, head, True)
+    for j in range(4):
+        back(send, j, 0)
+
     diff = (lax.broadcasted_iota(jnp.int32, (KT, UQ), 0) - lax.broadcasted_iota(jnp.int32, (KT, UQ), 1))
 
     def prep(idx, _):
         j, h = idx // G, idx % G
-        rows = pl.ds(pl.multiple_of(j * UQ, UQ), UQ)
-        cols = pl.ds(pl.multiple_of(h * HD, HD), HD)
+        rows, cols = rows_of(j), cols_of(h)
         prod = do_ref[rows, cols].astype(F32) * o_ref[rows, cols].astype(F32)
         d_scr[pl.ds(idx, 1), :] = jnp.sum(prod.T, axis=0, keepdims=True)
         dqt_scr[idx] = jnp.zeros((HD, UQ), F32)
+        qt_scr[idx] = q_ref[rows, cols].T
+        dot_scr[idx] = do_ref[rows, cols].T
         return 0
     lax.fori_loop(0, 4 * G, prep, 0)
-
-    def tile(tt, _):
-        t = NT - 1 - tt
-        krows = pl.ds(pl.multiple_of(t * KT, KT), KT)
-        dka[...] = jnp.zeros_like(dka)
-        dva[...] = jnp.zeros_like(dva)
-
-        def step(j, masked):
-            u = unit_of(i, j)
-            rows = pl.ds(pl.multiple_of(j * UQ, UQ), UQ)
+    last = [unit_of(i, j) // 2 for j in range(4)]
+
+    def keys(t):
+        return rd(t * KT, KT)
+
+    def dots(t, j, h):
+        s_scr[h] = dg(k_ref[keys(t), :], qt_scr[j * G + h], 1, 0)
+        dp_scr[h] = dg(v_ref[keys(t), :], dot_scr[j * G + h], 1, 0)
+
+    def first(n):
+        return tile_at(n + (last[3] < tile_at(n)).astype(jnp.int32))
+
+    for h in range(G):
+        dots(first(jnp.int32(0)), 3, h)
+
+    def tile(n, _):
+        t = tile_at(n)
+        krows = keys(t)
+        units = 0
+        for j in range(4):
+            units = units + (last[j] >= t).astype(jnp.int32)
+        pair = pl.ds(2 * t, 2)
+        dkv[pair] = jnp.zeros((2, 2, UQ, HD), F32)
+
+        def step(jj, _):
+            j = 3 - jj
+            wrap = jj + 1 == units
+            tn = jnp.where(wrap, first(n + 1), t)
+            jn = jnp.where(wrap, 3, j - 1)
+            off = unit_of(i, j) * UQ - t * KT
+            rows = rows_of(j)
             k = k_ref[krows, :]
-            v = v_ref[krows, :]
             dv = None
             dk = None
             for h in range(G):
@@ -477,42 +531,65 @@
                 cols = slice(h * HD, (h + 1) * HD)
                 q = q_ref[rows, cols]
                 do = do_ref[rows, cols]
-                s = dg(k, q, 1, 1) * C2
-                if masked:
-                    s = jnp.where(diff <= u * UQ - t * KT, s, NINF)
+                s = jnp.where(diff <= off, s_scr[h] * C2, NINF)
                 pb = jnp.exp2(s - l2_ref[pl.ds(idx, 1), :]).astype(BF)
-                dp = dg(v, do, 1, 1)
-                ds = (pb.astype(F32) * (dp - d_scr[pl.ds(idx, 1), :])).astype(BF)
+                ds = (pb.astype(F32) * (dp_scr[h] - d_scr[pl.ds(idx, 1), :])).astype(BF)
+                dots(tn, jn, h)
                 r1 = dg(pb, do, 1, 0)
                 r2 = dg(ds, q, 1, 0)
                 dv = r1 if dv is None else dv + r1
                 dk = r2 if dk is None else dk + r2
                 dqt_scr[idx] += dg(k, ds, 0, 0)
-            dva[...] += dv
-            dka[...] += dk
-
-        for jj in range(4):
-            j = 3 - jj
-            u = unit_of(i, j)
-            @pl.when(u // 2 > t)
-            def _():
-                step(j, False)
-
-            @pl.when(u // 2 == t)
-            def _():
-                step(j, True)
-        dk_ref[krows, :] = dka[...] * TSC
-        dv_ref[krows, :] = dva[...]
+            dkv[pair, 0] += dk.reshape(2, UQ, HD)
+            dkv[pair, 1] += dv.reshape(2, UQ, HD)
+            return 0
+        lax.fori_loop(0, units, step, 0)
+        over(n)
+        sums(n)
         return 0
     lax.fori_loop(0, NT, tile, 0)
 
-    def fin(idx, _):
+    def final(idx, _):
         j, h = idx // G, idx % G
-        rows = pl.ds(pl.multiple_of(j * UQ, UQ), UQ)
-        cols = pl.ds(pl.multiple_of(h * HD, HD), HD)
-        dq_ref[rows, cols] = (dqt_scr[idx] * TSC).T.astype(BF)
+        dq_ref[rows_of(j), cols_of(h)] = (dqt_scr[idx] * TSC).T.astype(BF)
         return 0
-    lax.fori_loop(0, 4 * G, fin, 0)
+    lax.fori_loop(0, 4 * G, final, 0)
+    for j in range(4):
+        back(send, j, 1)
+
+    def drain(n, _):
+        sums(n)
+        return 0
+    lax.fori_loop(NT, NT + LAGS[3], drain, 0)
+
+    def close(n, _):
+        for e in range(2):
+            u, _, slots, _, sends = item(n, e)
+            for r in range(4):
+                @pl.when(sends[r])
+                def _():
+                    link(n, e, u, slots, r).wait_send()
+        return 0
+    lax.fori_loop(0, NT, close, 0)
+    for n in range(4):
+        back_got(n)
+        for j in range(4):
+            back(sent, j, n)
+
+
+def attention_bwd(q, do, o, l2, k, v):
+    dma = pltpu.SemaphoreType.DMA
+    vm = pltpu.VMEM
+    sems = [dma((4, 2, 4)), dma((4, 2, 4))]
+    for n in ((32,), (2, 8), (2, 4), (2, 2)):
+        sems += [dma(n), dma(n)]
+    return pl.pallas_call(
+        bwd_kernel,
+        out_shape=(shape((256, 4 * G * HD), BF),) * 2 + (shape((256, 4 * HD), BF),) * 2, in_specs=[VM] * 6, out_specs=(VM,) * 4,
+        scratch_shapes=[vm((4 * UQ, G * HD), BF), vm((S // UQ, 2, UQ, HD), F32), vm((4 * G, UQ), F32), vm((4 * G, HD, UQ), F32),
+                        vm((4 * G, HD, UQ), BF), vm((4 * G, HD, UQ), BF), vm((G, KT, UQ), F32), vm((G, KT, UQ), F32),
+                        vm((32, 2, UQ, HD), F32), vm((2, 8, 2, UQ, HD), F32), vm((2, 4, 2, UQ, HD), F32), vm((2, 2, 2, UQ, HD), F32), vm((4, 2, UQ, HD), BF)] + sems,
+        compiler_params=params(62, 3), name='attention_bwd')(q, do, o, l2, k, v)
 
 
 def fwd_kernel(*refs):
@@ -520,24 +597,12 @@
     fwd_body(base_unit(grp, t), *refs)
 
 
-def bwd_kernel(*refs):
-    _, t, grp, _ = me()
-    bwd_body(base_unit(grp, t), *refs)
-
-
 def attention_fwd(q, k, v):
     return pl.pallas_call(
         fwd_kernel, out_shape=(shape((4 * UQ, G * HD), BF), shape((4 * G, UQ), F32)), in_specs=[VM] * 3, out_specs=(VM, VM),
-        scratch_shapes=[pltpu.VMEM((KT, UQ), F32), pltpu.VMEM((KT, UQ), F32), pltpu.VMEM((S, UQ), F32),
-                        pltpu.VMEM((S // KT, 8, UQ), F32), pltpu.VMEM((HD, UQ), F32)],
+        scratch_shapes=[pltpu.VMEM((KT, UQ), F32), pltpu.VMEM((NG - 1, KT, UQ), F32), pltpu.VMEM((S, UQ), F32),
+            pltpu.VMEM((S // CH, 8, UQ), F32), pltpu.VMEM((HD, UQ), F32), pltpu.VMEM((HD, S), BF), pltpu.VMEM((HD, UQ), BF)],
         compiler_params=params(60), name='attention_fwd')(q, k, v)
-
-
-def attention_bwd(q, do, o, l2, k, v):
-    return pl.pallas_call(
-        bwd_kernel, out_shape=(shape((4 * UQ, G * HD), BF), shape((S, HD), F32), shape((S, HD), F32)), in_specs=[VM] * 6, out_specs=(VM,) * 3,
-        scratch_shapes=[pltpu.VMEM((4 * G, UQ), F32), pltpu.VMEM((4 * G, HD, UQ), F32), pltpu.VMEM((KT, HD), F32), pltpu.VMEM((KT, HD), F32)],
-        compiler_params=params(60), name='attention_bwd')(q, do, o, l2, k, v)
 
 
 def solution(mesh):
@@ -551,8 +616,7 @@
         d_out = dg(dy_loc, w_out, 1, 1).astype(BF)
         q, do, k, v = spread(query, d_out, keys, values)
         o, l2 = attention_fwd(q, k, v)
-        dq, dk, dv = attention_bwd(q, do, o, l2, k, v)
-        ob, dqb, dkb, dvb = gather_back(o, dq, dk, dv)
+        ob, dqb, dkb, dvb = attention_bwd(q, do, o, l2, k, v)
         y_part = dg(ob, w_out, 1, 0)
         dx_part = dg(dqb, w_query, 1, 1) + dg(dkb, w_key, 1, 1) + dg(dvb, w_value, 1, 1)
         y_in, dx_in = pair_half(y_part, dx_part)

time: 395 us -> 316 us (0.80)
  Pallas kernels: 357 us -> 275 us
    pallas_call x2 -> x1, Pallas kernels: 201 us -> 127 us  [attention_bwd(): pl.pallas_call(bwd_kernel, out_shape=(shape((256, 4 * G * HD), BF),) * 2...]
    pallas_call x1, Pallas kernels: 78.5 us -> 63.2 us  [attention_fwd(): pl.pallas_call(fwd_kernel, out_shape=(shape((4 * UQ, G * HD), BF), shape(...]
    pallas_call x1, Pallas kernels: 5.78 us -> 13.3 us  [pair_half(): pl.pallas_call(pair_sum_kernel, out_shape=(shape((n // 2, d), y.dtype),)...]
where the time goes in v2:
time: 316 us; the launch traced here: 314 us
  Pallas kernels  275 us (87%)
  matrix products  21.3 us (7%)
  local copies, waits for them, and re-layouts  13.1 us (4%)
  other arithmetic  3.85 us (1%)
    pallas_call x1, Pallas kernels, attention_bwd(): pl.pallas_call(bwd_kernel, out_shape=(shape((256, 4 * G * HD), BF),) * 2...  127 us
    pallas_call x1, Pallas kernels, spread(): pl.pallas_call(spread_kernel, out_shape=(shape((4 * UQ, G * HD), BF),) *...  67 us
    pallas_call x1, Pallas kernels, attention_fwd(): pl.pallas_call(fwd_kernel, out_shape=(shape((4 * UQ, G * HD), BF), shape(...  63.2 us
    dot_general x8, matrix products, dg(): lax.dot_general(a, b, (((ca,), (cb,)), ((), ())), preferred_element_type=...  21.3 us
    pallas_call x1, Pallas kernels, pair_half(): pl.pallas_call(pair_sum_kernel, out_shape=(shape((n // 2, d), y.dtype),)...  13.3 us
    unnamed x44, local copies, waits for them, and re-layouts  13.1 us

profile of v2, /device:TPU:1, one launch (start us, length us, event | category | flops | bytes accessed | tf_op | source)
XLA Modules:
  0.0 314.4 jit_solution(18329893208722172483)
XLA Ops:
  0.6 0.0 copy-start.6
  0.6 1.1 copy-done.6
  1.8 1.1 copy-done.7
  2.9 4.4 %pair_gather.1 = (bf16[256,3072]{1,0:T(8,128)(2,1)S(1)}, bf16[256,3072]{1,0:T(8,128)(2,1)S(1)}) custom-call(bf16[128,3072]{1,0:T(8,128)(2,1)S(1)} %copy-done.6, bf16[128,3072]{1,0:T(8,128)(2,1)S(1)} %copy-done.7), custom_call_target="tpu_custom_call" | custom-call | tf_op jit(solution)/shard_map/pair_gather/pallas_call | solution.py:165
  7.3 0.0 copy-start.11
  7.4 0.0 slice-start.1
  7.4 0.0 slice-start.2
  7.4 6.4 %convolution_convert_fusion.1.q_ref = bf16[256,1536]{1,0:T(8,128)(2,1)S(1)} fusion(bf16[256,3072]{1,0:T(8,128)(2,1)S(1)} %get-tuple-element.16, bf16[3072,1536]{1,0:T(8,128)(2,1)} %param.8), kind=kOutput, calls=%fused_computation.3 | convolution fusion | flops 2416312320 | bytes 11796480 | tf_op jit(solution)/shard_map/dot_general | solution.py:29
  13.8 0.0 copy-done.11
  13.8 0.0 copy-start.9
  13.8 1.0 convolution_convert_fusion.2.v_ref
  14.8 0.9 copy-done.9
  15.7 1.0 convolution_convert_fusion.3.k_ref
  16.7 0.0 slice-done
  16.7 0.0 slice-done.1
  16.7 0.0 slice-done.2
  16.8 2.6 convolution_convert_fusion.do_ref
  19.4 67.0 %spread.1 = (bf16[1024,384]{1,0:T(8,128)(2,1)S(1)}, bf16[1024,384]{1,0:T(8,128)(2,1)S(1)}, bf16[16384,128]{1,0:T(8,128)(2,1)S(1)}, bf16[16384,128]{1,0:T(8,128)(2,1)S(1)}) custom-call(bf16[256,1536]{1,0:T(8,128)(2,1)S(1)} %convolution_convert_fusion.1.q_ref, bf16[256,1536]{1,0:T(8,128)(2,1)S(1)} %convolution_convert_fusion.do_ref, ...), custom_call_target="tpu_custom_call" | custom-call | tf_op jit(solution)/shard_map/spread/pallas_call | solution.py:276
  86.4 0.0 copy-start
  86.4 1.9 copy-done
  88.4 2.0 copy-done.1
  90.4 0.9 copy-done.3
  91.3 0.9 copy-done.8
  92.2 63.2 %attention_fwd.1 = (bf16[1024,384]{1,0:T(8,128)(2,1)}, f32[12,256]{1,0:T(8,128)}) custom-call(bf16[1024,384]{1,0:T(8,128)(2,1)} %copy-done.3, bf16[16384,128]{1,0:T(8,128)(2,1)} %copy-done, bf16[16384,128]{1,0:T(8,128)(2,1)} %copy-done.1), custom_call_target="tpu_custom_call" | custom-call | tf_op jit(solution)/shard_map/attention_fwd/pallas_call | solution.py:601
  155.3 127.4 %attention_bwd.1 = (bf16[256,1536]{1,0:T(8,128)(2,1)}, bf16[256,1536]{1,0:T(8,128)(2,1)}, bf16[256,512]{1,0:T(8,128)(2,1)}, bf16[256,512]{1,0:T(8,128)(2,1)}) custom-call(bf16[1024,384]{1,0:T(8,128)(2,1)} %copy-done.3, bf16[1024,384]{1,0:T(8,128)(2,1)} %copy-done.8, bf16[1024,384]{1,0:T(8,128)(2,1)} %get-tuple-element.22.o_ref, ...), custom_call_target="tpu_custom_call" | custom-call | tf_op jit(solution)/shard_map/attention_bwd/pallas_call | solution.py:586
  282.7 0.0 copy-start.10
  282.8 0.0 copy-start.14
  282.8 0.0 slice-start.3
  282.8 0.0 slice-start.4
  282.8 5.6 %fusion.1 = f32[256,3072]{1,0:T(8,128)S(1)} fusion(bf16[256,1536]{1,0:T(8,128)(2,1)} %get-tuple-element.25, bf16[3072,1536]{1,0:T(8,128)(2,1)} %param.8), kind=kOutput, calls=%fused_computation.9 | convolution fusion | flops 2415919104 | bytes 13369344 | tf_op jit(solution)/shard_map/dot_general | solution.py:29
  288.4 0.0 copy-done.10
  288.4 0.0 copy-done.14
  288.4 0.0 copy-start.12
  288.4 0.0 copy-start.13
  288.4 0.0 slice-start.5
  288.4 1.0 convolution_add_fusion.1
  289.5 1.6 copy-done.12
  291.0 0.0 copy-done.13
  291.0 1.0 convolution_add_fusion.dx_ref
  292.1 0.0 slice-done.3
  292.1 0.0 slice-done.4
  292.1 0.0 slice-done.5
  292.1 0.2 copy-done.15
  292.3 2.6 fusion.y_ref
  294.9 13.3 %pair_half.1 = (f32[128,3072]{1,0:T(8,128)S(1)}, f32[128,3072]{1,0:T(8,128)S(1)}) custom-call(f32[256,3072]{1,0:T(8,128)S(1)} %fusion.y_ref, f32[256,3072]{1,0:T(8,128)S(1)} %convolution_add_fusion.dx_ref), custom_call_target="tpu_custom_call" | custom-call | tf_op jit(solution)/shard_map/pair_half/pallas_call | solution.py:187
  308.2 1.2 copy-done.4
  309.4 1.2 copy-done.5
  310.6 3.8 %add_convert_fusion = (bf16[128,3072]{1,0:T(8,128)(2,1)}, bf16[128,3072]{1,0:T(8,128)(2,1)}) fusion(f32[128,3072]{1,0:T(8,128)} %copy-done.5, f32[256,3072]{1,0:T(8,128)S(1)} %convolution_add_fusion.dx_ref, s32[]{:T(128)S(6)} %select_n.4, f32[128,3072]{1,0:T(8,128)} %copy-done.4, f32[256,3072]{1,0:T(8,128)} %copy-done.2), kind=kLoop, calls=%fused_computation.4 | loop fusion | flops 1572864 | bytes 7864324 | tf_op jit(solution)/shard_map/convert_element_type | solution.py:627
  (12 shorter events, 0.0 us)
Async XLA Ops:
  0.6 1.1 copy-start.6
  1.8 1.1 copy-start.7
  2.9 13.8 %slice-start = ((s8[9437184]{0:T(1024)(128)(4,1)}), s8[4194304]{0:T(1024)(128)(4,1)S(1)}, s32[]{:S(2)}) async-start(s8[9437184]{0:T(1024)(128)(4,1)} %bitcast.16), calls=%async_computation | async-start | bytes 8388608
  7.3 6.5 %copy-start.11 = (bf16[3072,512]{1,0:T(8,128)(2,1)S(1)}, bf16[3072,512]{1,0:T(8,128)(2,1)}, u32[]{:S(2)}) copy-start(bf16[3072,512]{1,0:T(8,128)(2,1)} %param.10) | copy-start | bytes 9437188
  7.4 9.4 %slice-start.1 = ((s8[9437184]{0:T(1024)(128)(4,1)}), s8[4194304]{0:T(1024)(128)(4,1)S(1)}, s32[]{:S(2)}) async-start(s8[9437184]{0:T(1024)(128)(4,1)} %bitcast.16), calls=%async_computation.1 | async-start | bytes 8388608
  7.4 9.4 %slice-start.2 = ((s8[9437184]{0:T(1024)(128)(4,1)}), s8[1048576]{0:T(1024)(128)(4,1)S(1)}, s32[]{:S(2)}) async-start(s8[9437184]{0:T(1024)(128)(4,1)} %bitcast.16), calls=%async_computation.2 | async-start | bytes 2097152
  13.8 1.9 copy-start.9
  86.4 2.0 copy-start
  88.4 2.0 copy-start.1
  90.4 0.9 copy-start.3
  91.3 0.9 copy-start.8
  282.7 5.6 %copy-start.10 = (bf16[3072,512]{1,0:T(8,128)(2,1)S(1)}, bf16[3072,512]{1,0:T(8,128)(2,1)}, u32[]{:S(2)}) copy-start(bf16[3072,512]{1,0:T(8,128)(2,1)} %param.9) | copy-start | bytes 9437188
  282.8 5.6 %copy-start.14 = (bf16[256,512]{1,0:T(8,128)(2,1)S(1)}, bf16[256,512]{1,0:T(8,128)(2,1)}, u32[]{:S(2)}) copy-start(bf16[256,512]{1,0:T(8,128)(2,1)} %get-tuple-element.26) | copy-start | bytes 786436
  282.8 9.3 %slice-start.3 = ((s8[9437184]{0:T(1024)(128)(4,1)}), s8[4194304]{0:T(1024)(128)(4,1)S(1)}, s32[]{:S(2)}) async-start(s8[9437184]{0:T(1024)(128)(4,1)} %bitcast.18), calls=%async_computation.3 | async-start | bytes 8388608
  282.8 9.3 %slice-start.4 = ((s8[9437184]{0:T(1024)(128)(4,1)}), s8[4194304]{0:T(1024)(128)(4,1)S(1)}, s32[]{:S(2)}) async-start(s8[9437184]{0:T(1024)(128)(4,1)} %bitcast.18), calls=%async_computation.4 | async-start | bytes 8388608
  288.4 2.6 copy-start.12
  288.4 2.6 copy-start.13
  288.4 3.7 %slice-start.5 = ((s8[9437184]{0:T(1024)(128)(4,1)}), s8[1048576]{0:T(1024)(128)(4,1)S(1)}, s32[]{:S(2)}) async-start(s8[9437184]{0:T(1024)(128)(4,1)} %bitcast.18), calls=%async_computation.5 | async-start | bytes 2097152
  291.0 1.2 copy-start.15
  294.9 13.3 %copy-start.2 = (f32[256,3072]{1,0:T(8,128)}, f32[256,3072]{1,0:T(8,128)S(1)}, u32[]{:S(2)}) copy-start(f32[256,3072]{1,0:T(8,128)S(1)} %fusion.y_ref) | copy-start | bytes 9437188
  308.2 1.2 copy-start.4
  309.4 1.2 copy-start.5

commit v3 on v0

v3 whole, which is shorter than its diff:
```python
import functools

import jax
import jax.numpy as jnp
from jax import lax
from jax.experimental import pallas as pl
from jax.experimental.pallas import tpu as pltpu
from jax.sharding import PartitionSpec as P

HD = 128
PC = HD
S = 16384
G = 3
KT = 512
NG = 4
TG = KT * NG
UQ = 256
LAGS = (3, 7, 11, 15)
TSC = HD ** -0.5
C2 = TSC * 1.4426950408889634
NINF = -float('inf')
BF = jnp.bfloat16
F32 = jnp.float32


def dg(a, b, ca, cb):
    return lax.dot_general(a, b, (((ca,), (cb,)), ((), ())), preferred_element_type=F32)


def each(n, first=0):
    def run(body):
        def step(m, _):
            body(m)
            return 0
        lax.fori_loop(first, n, step, 0)
    return run


def mm(a, b):
    return dg(a, b, 1, 0)


def mt(a, b):
    return dg(a, b, 1, 1)


def tm(a, b):
    return dg(a, b, 0, 0)


def mirror(v, h):
    return v + h * (3 - 2 * v)


def turn(v, e):
    return v + e * (1 - 2 * v)


def split(c):
    co = (c // 16, (c // 4) % 4, c % 4)
    return tuple(mirror(v, v // 2) for v in co), tuple(v // 2 for v in co)


def chip(grp, head):
    z, y, x = (mirror(g, h) for g, h in zip(grp, head))
    return z * 16 + y * 4 + x


def base_tile(grp, k):
    return grp[0] * 4 + mirror(grp[1], k)


def tile_of(i, j):
    odd = j & 1
    return (j >> 1) * 16 + odd * 15 + (1 - 2 * odd) * i


def ahead(xa):
    row = lax.broadcasted_iota(jnp.int32, (KT, UQ), 0)
    col = lax.broadcasted_iota(jnp.int32, (KT, UQ), 1)
    quarter = row // PC
    piece = jnp.where(quarter == 0, 0, jnp.where(quarter == 1, 3, quarter - 1))
    late = col // PC
    return (piece - mirror(xa, late)) * PC + row % PC - col % PC


def flip(grp, mask):
    return tuple(1 - g if (mask >> d) & 1 else g for d, g in enumerate(grp))


def quad_block(grp, k, zs, par):
    return chip(grp, (zs, (zs + k) % 2, par))


def dev(c, t):
    return {'tp': t, 'cp': c}


def me():
    c, t = lax.axis_index('cp'), lax.axis_index('tp')
    grp, head = split(c)
    return c, t, grp, head


def line(n):
    return pl.ds(n, 1)


def rd(start, n):
    return pl.ds(pl.multiple_of(start, n), n)


def greet(c, t, grp, head):
    bar = pltpu.get_barrier_semaphore()
    for hh in range(8):
        for k in range(2):
            cc = chip(grp, (hh // 4, (hh // 2) % 2, hh % 2))

            @pl.when((cc != c) | (t != k))
            def _():
                pl.semaphore_signal(bar, 1, device_id=dev(cc, k), device_id_type=pl.DeviceIdType.MESH)
    for d in range(3):
        pl.semaphore_signal(bar, 1, device_id=dev(chip(flip(grp, 1 << d), head), t), device_id_type=pl.DeviceIdType.MESH)
    pl.semaphore_wait(bar, 18)


def rcopy(src, dst, ssem, rsem, cc, k):
    return pltpu.make_async_remote_copy(src_ref=src, dst_ref=dst, send_sem=ssem, recv_sem=rsem, device_id=dev(cc, k), device_id_type=pl.DeviceIdType.MESH)


def send(src, dst, ssem, rsem, cc, k, own):
    @pl.when(own)
    def _():
        pltpu.make_async_copy(src, dst, rsem).start()

    @pl.when(jnp.logical_not(own))
    def _():
        rcopy(src, dst, ssem, rsem, cc, k).start()


def sent(src, dst, ssem, rsem, cc, k, own):
    @pl.when(jnp.logical_not(own))
    def _():
        rcopy(src, dst, ssem, rsem, cc, k).wait_send()


def got(dst, rsem):
    pltpu.make_async_copy(dst, dst, rsem).wait()


def order(it):
    return [(it + r) % 3 for r in range(3)]


def below(dims):
    masks = [0]
    for d in dims:
        masks += [m | (1 << d) for m in masks]
    return masks


VM = pl.BlockSpec(memory_space=pltpu.VMEM)
ANY = pl.BlockSpec(memory_space=pl.ANY)
HB = pl.BlockSpec(memory_space=pltpu.HBM)


def params(kib, cid):
    return pltpu.CompilerParams(vmem_limit_bytes=kib * 1024, collective_id=cid, has_side_effects=True)


def shape(s, d):
    return jax.ShapeDtypeStruct(s, d)


def rows_of(j):
    return rd(j * UQ, UQ)


def cols_of(h):
    return rd(h * HD, HD)


PB = UQ


def forward(x_ref, dy_ref, wq, wk, wv, wo, qo_ref, doo_ref, ko_ref, vo_ref, o_ref, l2_ref, qt_scr, s_scr, ot_scr,
            kvq, dout, xp, dyp, wa, wb, m_scr, l_scr, mx_scr, xss, xrs, lsem, ss1, rs1, ss2, rs2, ss3, rs3):
    c, t, grp, head = me()
    zb, yb, xb = head
    par = xb
    k = (zb + yb) % 2
    i = base_tile(grp, t)
    outs = (ko_ref, vo_ref, qo_ref, doo_ref)
    half = x_ref.shape[0]
    kv_blocks, q_blocks = 2 * wk.shape[1] // PB, wq.shape[1] // PB

    def start(cp):
        cp.start()

    def wait(cp):
        cp.wait()

    def load(b, fn):
        for w, at, n in ((wk, 0, kv_blocks // 2), (wv, kv_blocks // 2, kv_blocks // 2), (wq, kv_blocks, q_blocks)):
            @pl.when((b >= at) & (b < at + n))
            def _():
                fn(pltpu.make_async_copy(w.at[:, rd((b - at) * PB, PB)], wa.at[b & 1], lsem.at[0, b & 1]))

    def load_out(b, fn):
        fn(pltpu.make_async_copy(wo.at[rd(b * PB, PB), :], wb.at[b & 1], lsem.at[1, b & 1]))

    def put(ref, b, r):
        ref[rd(t * half, half), rd(b * PB, PB)] = r[:half].astype(BF)
        ref[rd((1 - t) * half, half), rd(b * PB, PB)] = r[half:].astype(BF)

    def project(b):
        pltpu.make_async_copy(wa.at[b & 1], wa.at[b & 1], lsem.at[0, b & 1]).wait()
        put(kvq, b, mm(jnp.concatenate([x_ref[...], xp[...]], 0), wa[b & 1]))
        load(b + 2, start)

    def project_out(b):
        load_out(b, wait)
        put(dout, b, mt(jnp.concatenate([dy_ref[...], dyp[...]], 0), wb[b & 1]))

        @pl.when(b + 2 < q_blocks)
        def _():
            load_out(b + 2, start)

    for b in range(2):
        load(jnp.int32(b), start)
        load_out(b, start)
    greet(c, t, grp, head)
    swaps = [rcopy(src, dst, xss.at[n], xrs.at[n], c, 1 - t) for n, (src, dst) in enumerate(((x_ref, xp), (dy_ref, dyp)))]
    for cp in swaps:
        cp.start()

    def rows_q(zs, pr, e):
        return rd(mirror(zs, e) * UQ + turn(pr, e) * PC, PC)

    def rows_k(bb, e):
        q, half = bb // 4, (bb % 4) // 2
        return rd((q + e * (31 - 2 * q)) * KT + grp[2] * UQ + turn(half, e) * PC, PC)

    def first(fn, kinds, halves=(0, 1)):
        for e in halves:
            for hh in range(4):
                cc = chip(grp, (t, hh // 2, hh % 2))
                own = (cc == c) & (k == t)
                for n in kinds:
                    wide = HD if n < 2 else G * HD
                    at = (0, kv_blocks // 2 * PB, kv_blocks * PB, 0)[n] + hh * wide
                    src = (kvq, kvq, kvq, dout)[n].at[e * PC:(e + 1) * PC, at:at + wide]
                    dst = outs[n].at[rows_k(c, e) if n < 2 else rows_q(zb, par, e), :]
                    fn(src, dst, ss1.at[hh, n, e], rs1.at[zb * 2 + par, n, e], cc, k, own)

    def first_got(kinds, halves=(0, 1)):
        for zs in range(2):
            for pr in range(2):
                bb = quad_block(grp, t, zs, pr)
                for n in kinds:
                    for e in halves:
                        got(outs[n].at[rows_k(bb, e) if n < 2 else rows_q(zs, pr, e), :], rs1.at[zs * 2 + pr, n, e])

    def part(it, mask, kk):
        g2 = flip(grp, mask)
        r = rd(tile_of(base_tile(g2, kk), it // 2) * KT + g2[2] * UQ, UQ)
        return (ko_ref, vo_ref)[it % 2].at[r, :]

    def hop(it, r, mask):
        d = order(it)[r]
        ref = part(it, mask, t)
        m2 = mask | (1 << d)
        return rcopy(ref, ref, ss2.at[it, m2], rs2.at[it, m2], chip(flip(grp, 1 << d), head), t)

    def over(it, mask):
        ref = part(it, mask, t)
        return rcopy(ref, ref, ss3.at[it, mask], rs3.at[it, mask], c, 1 - t)

    def fresh(it, r):
        return [m | (1 << order(it)[r]) for m in below(order(it)[:r])]

    def arrived(it, r):
        for m in fresh(it, r):
            got(part(it, m, t), rs2.at[it, m])

    def relay(it, r):
        arrived(it, r)
        if r < 2:
            for m in below(order(it)[:r + 1]):
                hop(it, r + 1, m).start()
        for m in fresh(it, r):
            over(it, m).start()

    def ready(j):
        for it in (2 * j, 2 * j + 1):
            relay(it, 2)
        for it in (2 * j, 2 * j + 1):
            for m in range(8):
                got(part(it, m, 1 - t), rs3.at[it, m])

    swaps[0].wait_recv()
    each(kv_blocks)(project)
    first(send, (0, 1))
    each(kv_blocks + q_blocks, kv_blocks)(project)
    first(send, (2,))
    swaps[1].wait_recv()
    own_items = lambda e: range(4 * e, 4 * e + 4)
    for e in range(2):
        first_got((0, 1), (e,))
        for it in own_items(e):
            hop(it, 0, 0).start()
        for it in own_items(e):
            over(it, 0).start()
        each(q_blocks // 2 * (e + 1), q_blocks // 2 * e)(project_out)
        if e == 0:
            for it in own_items(0):
                relay(it, 0)
    for j in range(2):
        for it in (2 * j, 2 * j + 1):
            relay(it, 1)
        for it in (2 * j, 2 * j + 1):
            relay(it + 4, 0)
    first(send, (3,))
    first_got((2,))

    diff = ahead(grp[2])

    @each(4 * G)
    def _(idx):
        j, h = idx // G, idx % G
        qt_scr[idx] = qo_ref[rows_of(j), cols_of(h)].T

    def score(idx, g, e, masked):
        kt = g * NG + e
        s = mm(ko_ref[rd(kt * KT, KT), :], qt_scr[idx])
        if masked:
            s = jnp.where(diff <= (tile_of(i, idx // G) - kt) * KT, s, NINF)
        s_scr[e] = s
        return jnp.max(s.reshape(KT // 8, 8, UQ), axis=0)

    def top(ms):
        m = ms[0]
        for x in ms[1:]:
            m = jnp.maximum(m, x)
        return jnp.max(m, axis=0, keepdims=True) * C2

    def step(idx, g, nidx, ng, masked):
        mo = m_scr[line(idx), :]
        mn = jnp.maximum(mo, mx_scr[:])
        fade = jnp.exp2(mo - mn)
        l = l_scr[idx] * fade
        acc = None
        ms = []
        for e in range(NG):
            p = jnp.exp2(s_scr[e] * C2 - mn)
            l = l + jnp.sum(p.reshape(KT // 8, 8, UQ), axis=0)
            r = tm(vo_ref[rd((g * NG + e) * KT, KT), :], p.astype(BF))
            acc = r if acc is None else acc + r
            ms.append(score(nidx, ng, e, masked))
        ot_scr[idx] = ot_scr[idx] * fade + acc
        m_scr[line(idx), :] = mn
        l_scr[idx] = l
        mx_scr[:] = top(ms)

    ends = [tile_of(i, j) // NG for j in range(4)]
    per = S // TG // 4
    ready(0)
    for j in range(4):
        for h in range(G):
            ot_scr[j * G + h] = jnp.zeros((HD, UQ), F32)
            l_scr[j * G + h] = jnp.zeros((8, UQ), F32)
    m_scr[:] = jnp.full(m_scr.shape, jnp.finfo(F32).min)
    mx_scr[:] = top([score(0, 0, e, True) for e in range(NG)])

    @each(4)
    def _(a):
        @each(4 * G, a * G)
        def _(idx):
            j, h = idx // G, idx % G
            for jn in range(1, 4):
                @pl.when((a == jn - 1) & (idx == 4 * G - 1))
                def _():
                    ready(jn)

                if jn > 1:
                    @pl.when((a == 0) & (idx == G * jn - G))
                    def _():
                        relay(2 * jn, 1)
                        relay(2 * jn + 1, 1)
            end = ends[0] * (a == 0) + ends[1] * (a == 1) + ends[2] * (a == 2) + ends[3] * (a == 3)
            stop = jnp.where(j == a, end + 1, per * (a + 1))

            @each(stop, per * a)
            def _(g):
                more = g + 1 < stop
                wrap = idx == 4 * G - 1
                nidx = jnp.where(more, idx, jnp.where(wrap, jnp.minimum(a + 1, 3) * G, idx + 1))
                ng = jnp.where(more, g + 1, jnp.where(wrap, jnp.minimum(a + 1, 3), a) * per)
                masked = ng == tile_of(i, nidx // G) // NG

                @pl.when(masked)
                def _():
                    step(idx, g, nidx, ng, True)

                @pl.when(jnp.logical_not(masked))
                def _():
                    step(idx, g, nidx, ng, False)

            @pl.when(j == a)
            def _():
                lt = jnp.sum(l_scr[idx], axis=0, keepdims=True)
                l2_ref[line(idx), :] = m_scr[line(idx), :] + jnp.log2(lt)
                o_ref[rows_of(j), cols_of(h)] = (ot_scr[idx] / lt).T.astype(BF)

    first_got((3,))

    def finish():
        for it in range(8):
            for r in range(3):
                for m in below(order(it)[:r]):
                    hop(it, r, m).wait_send()
            for m in range(8):
                over(it, m).wait_send()
        first(sent, (0, 1, 2, 3))
        for cp in swaps:
            cp.wait_send()
    return finish


RES = (0, 4 * G, 8 * G, 8 * G + 4)


def owners(t):
    j = t >> 3
    odd, hi = j & 1, j >> 1
    h = (1 - 2 * odd) * t + odd * (15 + 16 * hi) - (1 - odd) * 16 * hi
    za, yk = h >> 2, h & 3
    k = yk >> 1
    return j, k, za, mirror(yk, k)


def backward(q_ref, do_ref, o_ref, l2_ref, k_ref, v_ref, res_ref,
             qt_scr, s_scr, dqt_scr, dkv, d_scr, dot_scr, dp_scr,
               rb0, rb1, rb2, rb3, fin, ssb, rsb, ss0, rs0, ss1, rs1, ss2, rs2, ss3, rs3):
    c, t_me, grp, head = me()
    zb, yb, xb = head
    hm = yb * 2 + xb
    i = base_tile(grp, t_me)
    NT = S // KT
    nbrs = [chip(flip(grp, 1 << d), head) for d in range(3)]

    def back(fn, j, n):
        zs = ((j + 1) // 2) % 2
        half = j // 2
        for e in range(2):
            par = turn(e, half)
            cc = quad_block(grp, t_me, zs, par)
            own = (cc == c) & (zb == t_me)
            wide = G * HD if n < 2 else HD
            if n < 2:
                src = o_ref.at[rd(j * UQ + e * PC, PC), :]
            else:
                src = fin.at[j, n - 2, e * PC:(e + 1) * PC, :]
            dst = res_ref.at[rd(half * PC, PC), pl.ds(pl.multiple_of(RES[n] * HD + hm * wide, HD), wide)]
            fn(src, dst, ssb.at[j, e, n], rsb.at[hm, half, n], cc, zb, own)

    def back_got(n):
        wide = G * HD if n < 2 else HD
        for hh in range(4):
            for half in range(2):
                got(res_ref.at[half * PC:(half + 1) * PC, RES[n] * HD + hh * wide:RES[n] * HD + (hh + 1) * wide], rsb.at[hh, half, n])

    def item(n, e):
        t = tile_at(n)
        j, k, za, ya = owners(t)
        hi = j >> 1
        half = (e + j) & 1
        same = [za == grp[0], ya == grp[1], half == grp[2]]
        if e:
            same = same[::-1]
            slots = [(j * 2 + 1) * 4 + za * 2 + ya, hi * 4 + za * 2 + ya, hi * 2 + za, hi]
        else:
            slots = [j * 8 + za * 2 + ya, j * 2 + ya, j, hi]
        there = [k == t_me]
        for d in range(3):
            there.append(there[d] & same[d])
        sends = [k != t_me] + [there[d] & jnp.logical_not(same[d]) for d in range(3)]
        return 2 * t + half, j, slots, there, sends

    def link(n, e, u, slots, r):
        if r == 0:
            return rcopy(dkv.at[u], rb0.at[slots[0]], ss0.at[slots[0]], rs0.at[slots[0]], c, 1 - t_me)
        rb, ss, rs = ((rb1, ss1, rs1), (rb2, ss2, rs2), (rb3, ss3, rs3))[r - 1]
        return rcopy(rb0.at[slots[0]], rb.at[e, slots[r]], ss.at[e, slots[r]], rs.at[e, slots[r]], nbrs[3 - r if e else r - 1], t_me)

    def over(n):
        for e in range(2):
            u, _, slots, _, sends = item(n, e)

            @pl.when(sends[0])
            def _():
                link(n, e, u, slots, 0).start()

    def stage(n, r):
        for e in range(2):
            u, j, slots, there, sends = item(n, e)
            acc = rb0.at[slots[0]]

            @pl.when(there[r])
            def _():
                if r == 0:
                    got(acc, rs0.at[slots[0]])
                    acc[...] = acc[...] + dkv[u]
                else:
                    rb, rs = ((rb1, rs1), (rb2, rs2), (rb3, rs3))[r - 1]
                    new = rb.at[e, slots[r]]
                    got(new, rs.at[e, slots[r]])
                    if r < 3:
                        acc[...] = acc[...] + new[...]
                    else:
                        fin[j, 0] = ((acc[0] + new[0]) * TSC).T.astype(BF)
                        fin[j, 1] = (acc[1] + new[1]).T.astype(BF)
                        back(send, j, 2)
                        back(send, j, 3)
            if r < 3:
                @pl.when(sends[r + 1])
                def _():
                    link(n, e, u, slots, r + 1).start()

    def tile_at(n):
        n = jnp.minimum(n, NT - 1)
        b, a, w = n >> 3, (n >> 1) & 3, n & 1
        low = 4 * (b + 1 - 2 * (b & 1)) + a + 2 - 4 * (a >> 1)
        return (1 - w) * (31 - 4 * b - a) + w * low

    def sums(n):
        for r in range(4):
            m = n - LAGS[r]

            @pl.when((m >= 0) & (m < NT))
            def _():
                stage(m, r)

    for j in range(4):
        back(send, j, 0)

    diff = ahead(grp[2])

    @each(4 * G)
    def _(idx):
        j, h = idx // G, idx % G
        rows, cols = rows_of(j), cols_of(h)
        prod = do_ref[rows, cols].astype(F32) * o_ref[rows, cols].astype(F32)
        d_scr[line(idx), :] = jnp.sum(prod.T, axis=0, keepdims=True)
        dqt_scr[idx] = jnp.zeros((HD, UQ), F32)
        dot_scr[idx] = do_ref[rows, cols].T
    last = [tile_of(i, j) for j in range(4)]

    def keys(t):
        return rd(t * KT, KT)

    def dots(t, j, h):
        s_scr[h] = mm(k_ref[keys(t), :], qt_scr[j * G + h])
        dp_scr[h] = mm(v_ref[keys(t), :], dot_scr[j * G + h])

    def first(n):
        return tile_at(n + (last[3] < tile_at(n)).astype(jnp.int32))

    for h in range(G):
        dots(first(jnp.int32(0)), 3, h)

    @each(NT)
    def _(n):
        t = tile_at(n)
        krows = keys(t)
        units = 0
        for j in range(4):
            units = units + (last[j] >= t).astype(jnp.int32)
        dkv[pl.ds(2 * t, 2)] = jnp.zeros((2, 2, HD, UQ), F32)

        @each(units)
        def _(jj):
            j = 3 - jj
            wrap = jj + 1 == units
            tn = jnp.where(wrap, first(n + 1), t)
            jn = jnp.where(wrap, 3, j - 1)
            off = (tile_of(i, j) - t) * KT
            k = k_ref[krows, :]
            dv = None
            dk = None
            for h in range(G):
                idx = j * G + h
                s = jnp.where(diff <= off, s_scr[h] * C2, NINF)
                pb = jnp.exp2(s - l2_ref[line(idx), :]).astype(BF)
                ds = (pb.astype(F32) * (dp_scr[h] - d_scr[line(idx), :])).astype(BF)
                dots(tn, jn, h)
                r1 = mt(dot_scr[idx], pb)
                r2 = mt(qt_scr[idx], ds)
                dv = r1 if dv is None else dv + r1
                dk = r2 if dk is None else dk + r2
                dqt_scr[idx] += tm(k, ds)
            for e in range(2):
                dkv[2 * t + e, 0] += dk[:, e * UQ:(e + 1) * UQ]
                dkv[2 * t + e, 1] += dv[:, e * UQ:(e + 1) * UQ]
        over(n)
        sums(n)

    back_got(0)
    for j in range(4):
        back(sent, j, 0)

    @each(4 * G)
    def _(idx):
        j, h = idx // G, idx % G
        o_ref[rows_of(j), cols_of(h)] = (dqt_scr[idx] * TSC).T.astype(BF)
    for j in range(4):
        back(send, j, 1)

    @each(NT + LAGS[3], NT)
    def _(n):
        sums(n)

    @each(NT)
    def _(n):
        for e in range(2):
            u, _, slots, _, sends = item(n, e)
            for r in range(4):
                @pl.when(sends[r])
                def _():
                    link(n, e, u, slots, r).wait_send()
    for n in range(1, 4):
        back_got(n)
        for j in range(4):
            back(sent, j, n)


def attention_kernel(x_ref, dy_ref, wq, wk, wv, wo, res_ref, qo, doo, ko, vo, o, l2, qt, s_scr, acc, *scr):
    finish = forward(x_ref, dy_ref, wq, wk, wv, wo, qo, doo, ko, vo, o, l2, qt, s_scr, acc, *scr[:18])
    backward(qo, doo, o, l2, ko, vo, res_ref, qt, s_scr, acc, *scr[18:])
    finish()


def attention(x, dy, wq, wk, wv, wo):
    dma = pltpu.SemaphoreType.DMA
    vm = pltpu.VMEM
    both = lambda *m: [dma(m)] * 2
    n, d = x.shape
    wide = vm((4 * UQ, G * HD), BF)
    turned = vm((4 * G, HD, UQ), BF)
    shared = [wide, wide, vm((S, HD), BF), vm((S, HD), BF), wide, vm((4 * G, UQ), F32), turned, vm((NG, KT, UQ), F32), vm((4 * G, HD, UQ), F32)]
    fwd = [vm((2 * n, 2 * wk.shape[1] + wq.shape[1]), BF), vm((2 * n, wq.shape[1]), BF), vm((n, d), BF), vm((n, d), BF),
           vm((2, d, PB), BF), vm((2, PB, d), BF), vm((4 * G, UQ), F32), vm((4 * G, 8, UQ), F32), vm((1, UQ), F32), *both(2), dma((2, 2)),
           *both(4, 4, 2), *both(8, 8), *both(8, 8)]
    bwd = [vm((S // UQ, 2, HD, UQ), F32), vm((4 * G, UQ), F32), turned,
           vm((G, KT, UQ), F32), vm((32, 2, HD, UQ), F32), vm((2, 8, 2, HD, UQ), F32),
           vm((2, 4, 2, HD, UQ), F32), vm((2, 2, 2, HD, UQ), F32), vm((4, 2, UQ, HD), BF), *both(4, 2, 4),
           *both(32), *both(2, 8), *both(2, 4), *both(2, 2)]
    return pl.pallas_call(
        attention_kernel,
        out_shape=shape((2 * n, 2 * wq.shape[1] + 2 * wk.shape[1]), BF), in_specs=[VM] * 2 + [ANY] * 4, out_specs=VM,
        scratch_shapes=shared + fwd + bwd, compiler_params=params(65472, 2), name='attention')(x, dy, wq, wk, wv, wo)


NB = 512
DEEP = 4


def out_kernel(res_ref, wo, wq, wk, wv, y_own, y_in, dx_own, dx_in, bo, bq, bk, bv, away, lsem, ssem, rsem):
    c, t = lax.axis_index('cp'), lax.axis_index('tp')
    rows, width = y_own.shape
    blocks = width // NB

    def cols(b):
        return rd(b * NB, NB)

    def part(n, wide):
        return res_ref[:, RES[n] * HD:RES[n] * HD + wide]

    def loads(n, b, fn):
        s = b % DEEP
        if n == 0:
            fn(pltpu.make_async_copy(wo.at[:, cols(b)], bo.at[s], lsem.at[0, s]))
        else:
            for m, (w, buf) in enumerate(((wq, bq), (wk, bk), (wv, bv))):
                fn(pltpu.make_async_copy(w.at[cols(b), :], buf.at[s], lsem.at[1 + m, s]))

    def start(cp):
        cp.start()

    def wait(cp):
        cp.wait()

    for n in range(2):
        for b in range(DEEP):
            loads(n, b, start)
    bar = pltpu.get_barrier_semaphore()
    pl.semaphore_signal(bar, 1, device_id=dev(c, 1 - t), device_id_type=pl.DeviceIdType.MESH)
    pl.semaphore_wait(bar, 1)

    def swap(n, b):
        return rcopy(away.at[n, b], (y_in, dx_in)[n].at[:, cols(b)], ssem.at[n, b], rsem.at[n, b], c, 1 - t)

    def block(n, b):
        s = b % DEEP
        loads(n, b, wait)
        if n == 0:
            r = mm(part(0, bo.shape[1]), bo[s])
        else:
            r = mt(part(1, bq.shape[2]), bq[s]) + mt(part(2, bk.shape[2]), bk[s]) + mt(part(3, bv.shape[2]), bv[s])

        own = (y_own, dx_own)[n]

        @pl.when(t == 0)
        def _():
            own[:, cols(b)] = r[:rows]
            away[n, b] = r[rows:]

        @pl.when(t == 1)
        def _():
            own[:, cols(b)] = r[rows:]
            away[n, b] = r[:rows]
        swap(n, b).start()

        @pl.when(b + DEEP < blocks)
        def _():
            loads(n, b + DEEP, start)

    for n in range(2):
        @each(blocks)
        def _(b):
            block(n, b)

    @each(blocks)
    def _(b):
        swap(0, b).wait()
        swap(1, b).wait()


def outputs(res, wo, wq, wk, wv):
    n, width = res.shape[0] // 2, wo.shape[1]
    b = width // NB
    dma = pltpu.SemaphoreType.DMA
    vm = pltpu.VMEM
    f = pl.pallas_call(
        out_kernel, out_shape=(shape((n, width), F32),) * 4, in_specs=[VM] + [HB] * 4, out_specs=(VM,) * 4,
        scratch_shapes=[vm((DEEP, wo.shape[0], NB), BF), vm((DEEP, NB, wq.shape[1]), BF), vm((DEEP, NB, wk.shape[1]), BF),
                        vm((DEEP, NB, wv.shape[1]), BF), vm((2, b, n, NB), F32), dma((4, DEEP)), dma((2, b)), dma((2, b))],
        compiler_params=params(46080, 1), name='outputs')
    y_own, y_in, dx_own, dx_in = f(res, wo, wq, wk, wv)
    return (y_own + y_in).astype(BF), (dx_own + dx_in).astype(BF)


def solution(mesh):
    row_spec = P(('dp', 'cp', 'tp'), None)

    def local_step(x_blk, dy_blk, w_query, w_key, w_value, w_out):
        res = attention(x_blk, dy_blk, w_query, w_key, w_value, w_out)
        return outputs(res, w_out, w_query, w_key, w_value)

    return jax.shard_map(local_step, mesh=mesh, in_specs=(row_spec, row_spec, P(None, 'tp'), P(None, 'tp'), P(None, 'tp'), P('tp', None)), out_specs=(row_spec, row_spec), check_vma=False)
```

time: 3000 us -> 213 us (0.07)
  matrix products: 1590 us -> 0 us
  waiting for transfers between devices: 1100 us -> 0 us
  other arithmetic: 256 us -> 1.53 us
  Pallas kernels: 0 us -> 208 us
  local copies, waits for them, and re-layouts: 35.3 us -> 1.58 us
    dot_general x104 -> x0, matrix products: 1590 us -> none  [the longest x16 407 us: block_step(): jnp.einsum('hgqk,qhgd->khd', d_score, q_blk, preferred_element_type=jnp.f...]
    reduce_scatter x4 -> x0, waiting for transfers between devices: 886 us -> none  [the longest x1 448 us: local_step(): lax.psum_scatter(dv_part, 'cp', scatter_dimension=0, tiled=True)]
    all_gather x4 -> x0, waiting for transfers between devices: 213 us -> none  [the longest x1 107 us: local_step(): keys_all = lax.all_gather(keys_loc, 'cp', axis=0, tiled=True)]
    pallas_call x0 -> x2, Pallas kernels: none -> 208 us  [the longest x1 190 us: attention(): pl.pallas_call(attention_kernel, out_shape=shape((2 * n, 2 * wq.shape[1]...]
    convert_element_type x20 -> x1, other arithmetic: 149 us -> 1.53 us  [outputs(): return ((y_own + y_in).astype(BF), (dx_own + dx_in).astype(BF))]
    reduce_sum x16 -> x0, other arithmetic: 102 us -> none  [block_step(): log_norm = jax.nn.logsumexp(scores, axis=-1, keepdims=True)]
  transfers between devices with their start and end apart: 8 -> 0, of which waited for: 8 -> 0; matrix products, arithmetic and copies ran while one was open for 2% -> 0% of each run, Pallas kernels for 0% -> 0%
where the time goes in v3:
time: 213 us; the launch traced here: 212 us
  Pallas kernels  208 us (98%)
    pallas_call x1, Pallas kernels, attention(): pl.pallas_call(attention_kernel, out_shape=shape((2 * n, 2 * wq.shape[1]...  190 us
    pallas_call x1, Pallas kernels, outputs(): y_own, y_in, dx_own, dx_in = f(res, wo, wq, wk, wv)  18.3 us

profile of v3, /device:TPU:1, one launch (start us, length us, event | category | flops | bytes accessed | tf_op | source)
XLA Modules:
  0.0 211.7 jit_solution(7717320326139980109)
XLA Ops:
  0.6 189.6 %attention.1.res_ref = bf16[256,4096]{1,0:T(8,128)(2,1)} custom-call(bf16[128,3072]{1,0:T(8,128)(2,1)} %x_ref.1, bf16[128,3072]{1,0:T(8,128)(2,1)} %dy_ref.1, bf16[3072,1536]{1,0:T(8,128)(2,1)} %wq.3, bf16[3072,512]{1,0:T(8,128)(2,1)} %wk.3, bf16[3072,512]{1,0:T(8,128)(2,1)} %wv.3, bf16[1536,3072]{1,0:T(8,128)(2,1)} %wo.3), custom_call_target="tpu_custom_call" | custom-call | tf_op jit(solution)/shard_map/attention/pallas_call | solution.py:658
  190.2 0.0 copy-start
  190.3 1.6 copy-done
  191.8 18.3 %outputs.1 = (f32[128,3072]{1,0:T(8,128)S(1)}, f32[128,3072]{1,0:T(8,128)S(1)}, f32[128,3072]{1,0:T(8,128)S(1)}, f32[128,3072]{1,0:T(8,128)S(1)}) custom-call(bf16[256,4096]{1,0:T(8,128)(2,1)S(1)} %copy-done, bf16[1536,3072]{1,0:T(8,128)(2,1)} %wo.3, bf16[3072,1536]{1,0:T(8,128)(2,1)} %wq.3, bf16[3072,512]{1,0:T(8,128)(2,1)} %wk.3, bf16[3072,512]{1,0:T(8,128)(2,1)} %wv.3), custom_call_target="tpu_custom_call" | custom-call | tf_op jit(solution)/shard_map/outputs/pallas_call | solution.py:749
  210.2 1.5 add_convert_fusion
Async XLA Ops:
  190.2 1.6 copy-start

commit v4 on v3

--- a/solution.py
+++ b/solution.py
@@ -70,9 +70,13 @@
     return grp[0] * 4 + mirror(grp[1], k)
 
 
+def bits(n):
+    return n >> 1, n & 1
+
+
 def tile_of(i, j):
-    odd = j & 1
-    return (j >> 1) * 16 + odd * 15 + (1 - 2 * odd) * i
+    hi, odd = bits(j)
+    return hi * 16 + odd * 15 + i - 2 * odd * i
 
 
 def ahead(xa):
@@ -106,6 +110,10 @@
     return pl.ds(n, 1)
 
 
+def cuts(n):
+    return [pl.ds(m, n // 4) for m in range(0, n, n // 4)]
+
+
 def rd(start, n):
     return pl.ds(pl.multiple_of(start, n), n)
 
@@ -184,8 +192,9 @@
 
 
 def forward(x_ref, dy_ref, wq, wk, wv, wo, qo_ref, doo_ref, ko_ref, vo_ref, o_ref, l2_ref, qt_scr, s_scr, ot_scr,
-            kvq, dout, xp, dyp, wa, wb, m_scr, l_scr, mx_scr, xss, xrs, lsem, ss1, rs1, ss2, rs2, ss3, rs3):
+            wa, wb, lsem, kvq, dout, xp, dyp, m_scr, l_scr, mx_scr, xss, xrs, ss1, rs1, ss2, rs2, ss3, rs3):
     c, t, grp, head = me()
+    peer = 1 - t
     zb, yb, xb = head
     par = xb
     k = (zb + yb) % 2
@@ -194,43 +203,39 @@
     half = x_ref.shape[0]
     kv_blocks, q_blocks = 2 * wk.shape[1] // PB, wq.shape[1] // PB
 
-    def start(cp):
-        cp.start()
-
-    def wait(cp):
-        cp.wait()
-
-    def load(b, fn):
+    def load(b):
         for w, at, n in ((wk, 0, kv_blocks // 2), (wv, kv_blocks // 2, kv_blocks // 2), (wq, kv_blocks, q_blocks)):
             @pl.when((b >= at) & (b < at + n))
             def _():
-                fn(pltpu.make_async_copy(w.at[:, rd((b - at) * PB, PB)], wa.at[b & 1], lsem.at[0, b & 1]))
-
-    def load_out(b, fn):
-        fn(pltpu.make_async_copy(wo.at[rd(b * PB, PB), :], wb.at[b & 1], lsem.at[1, b & 1]))
+                for rows in cuts(w.shape[0]):
+                    pltpu.make_async_copy(w.at[rows, rd((b - at) * PB, PB)], wa.at[b & 1, rows, :], lsem.at[0, b & 1]).start()
+
+    def load_out(b):
+        for cols in cuts(wo.shape[1]):
+            pltpu.make_async_copy(wo.at[rd(b * PB, PB), cols], wb.at[b & 1, :, cols], lsem.at[1, b & 1]).start()
 
     def put(ref, b, r):
         ref[rd(t * half, half), rd(b * PB, PB)] = r[:half].astype(BF)
-        ref[rd((1 - t) * half, half), rd(b * PB, PB)] = r[half:].astype(BF)
+        ref[rd(peer * half, half), rd(b * PB, PB)] = r[half:].astype(BF)
 
     def project(b):
-        pltpu.make_async_copy(wa.at[b & 1], wa.at[b & 1], lsem.at[0, b & 1]).wait()
+        got(wa.at[b & 1], lsem.at[0, b & 1])
         put(kvq, b, mm(jnp.concatenate([x_ref[...], xp[...]], 0), wa[b & 1]))
-        load(b + 2, start)
+        load(b + 2)
 
     def project_out(b):
-        load_out(b, wait)
+        got(wb.at[b & 1], lsem.at[1, b & 1])
         put(dout, b, mt(jnp.concatenate([dy_ref[...], dyp[...]], 0), wb[b & 1]))
 
         @pl.when(b + 2 < q_blocks)
         def _():
-            load_out(b + 2, start)
+            load_out(b + 2)
 
     for b in range(2):
-        load(jnp.int32(b), start)
-        load_out(b, start)
+        load(jnp.int32(b))
+        load_out(b)
     greet(c, t, grp, head)
-    swaps = [rcopy(src, dst, xss.at[n], xrs.at[n], c, 1 - t) for n, (src, dst) in enumerate(((x_ref, xp), (dy_ref, dyp)))]
+    swaps = [rcopy(src, dst, xss.at[n], xrs.at[n], c, peer) for n, (src, dst) in enumerate(((x_ref, xp), (dy_ref, dyp)))]
     for cp in swaps:
         cp.start()
 
@@ -266,6 +271,9 @@
         r = rd(tile_of(base_tile(g2, kk), it // 2) * KT + g2[2] * UQ, UQ)
         return (ko_ref, vo_ref)[it % 2].at[r, :]
 
+    def pair(j):
+        return 2 * j, 2 * j + 1
+
     def hop(it, r, mask):
         d = order(it)[r]
         ref = part(it, mask, t)
@@ -274,7 +282,7 @@
 
     def over(it, mask):
         ref = part(it, mask, t)
-        return rcopy(ref, ref, ss3.at[it, mask], rs3.at[it, mask], c, 1 - t)
+        return rcopy(ref, ref, ss3.at[it, mask], rs3.at[it, mask], c, peer)
 
     def fresh(it, r):
         return [m | (1 << order(it)[r]) for m in below(order(it)[:r])]
@@ -292,11 +300,11 @@
             over(it, m).start()
 
     def ready(j):
-        for it in (2 * j, 2 * j + 1):
+        for it in pair(j):
             relay(it, 2)
-        for it in (2 * j, 2 * j + 1):
+        for it in pair(j):
             for m in range(8):
-                got(part(it, m, 1 - t), rs3.at[it, m])
+                got(part(it, m, peer), rs3.at[it, m])
 
     swaps[0].wait_recv()
     each(kv_blocks)(project)
@@ -304,21 +312,21 @@
     each(kv_blocks + q_blocks, kv_blocks)(project)
     first(send, (2,))
     swaps[1].wait_recv()
-    own_items = lambda e: range(4 * e, 4 * e + 4)
     for e in range(2):
         first_got((0, 1), (e,))
-        for it in own_items(e):
+        items = pair(2 * e) + pair(2 * e + 1)
+        for it in items:
             hop(it, 0, 0).start()
-        for it in own_items(e):
+        for it in items:
             over(it, 0).start()
         each(q_blocks // 2 * (e + 1), q_blocks // 2 * e)(project_out)
         if e == 0:
-            for it in own_items(0):
+            for it in items:
                 relay(it, 0)
     for j in range(2):
-        for it in (2 * j, 2 * j + 1):
+        for it in pair(j):
             relay(it, 1)
-        for it in (2 * j, 2 * j + 1):
+        for it in pair(j):
             relay(it + 4, 0)
     first(send, (3,))
     first_got((2,))
@@ -385,9 +393,9 @@
                 if jn > 1:
                     @pl.when((a == 0) & (idx == G * jn - G))
                     def _():
-                        relay(2 * jn, 1)
-                        relay(2 * jn + 1, 1)
-            end = ends[0] * (a == 0) + ends[1] * (a == 1) + ends[2] * (a == 2) + ends[3] * (a == 3)
+                        for it in pair(jn):
+                            relay(it, 1)
+            end = sum(x * (a == m) for m, x in enumerate(ends))
             stop = jnp.where(j == a, end + 1, per * (a + 1))
 
             @each(stop, per * a)
@@ -427,20 +435,20 @@
     return finish
 
 
-RES = (0, 4 * G, 8 * G, 8 * G + 4)
+RES = (0, 4 * G, 0, 4)
 
 
 def owners(t):
     j = t >> 3
-    odd, hi = j & 1, j >> 1
-    h = (1 - 2 * odd) * t + odd * (15 + 16 * hi) - (1 - odd) * 16 * hi
+    hi, odd = bits(j)
+    h = tile_of(t, j) - hi * (1 - odd) * 32
     za, yk = h >> 2, h & 3
     k = yk >> 1
     return j, k, za, mirror(yk, k)
 
 
-def backward(q_ref, do_ref, o_ref, l2_ref, k_ref, v_ref, res_ref,
-             qt_scr, s_scr, dqt_scr, dkv, d_scr, dot_scr, dp_scr,
+def backward(q_ref, do_ref, o_ref, l2_ref, k_ref, v_ref, wq, wo, kvb_ref, y_ref, dx_ref,
+             qt_scr, s_scr, dqt_scr, wa, wb, lsem, res, osem, dkv, d_scr, dot_scr, dp_scr,
                rb0, rb1, rb2, rb3, fin, ssb, rsb, ss0, rs0, ss1, rs1, ss2, rs2, ss3, rs3):
     c, t_me, grp, head = me()
     zb, yb, xb = head
@@ -448,6 +456,8 @@
     i = base_tile(grp, t_me)
     NT = S // KT
     nbrs = [chip(flip(grp, 1 << d), head) for d in range(3)]
+
+    backs = (res, res, kvb_ref, kvb_ref)
 
     def back(fn, j, n):
         zs = ((j + 1) // 2) % 2
@@ -461,18 +471,21 @@
                 src = o_ref.at[rd(j * UQ + e * PC, PC), :]
             else:
                 src = fin.at[j, n - 2, e * PC:(e + 1) * PC, :]
-            dst = res_ref.at[rd(half * PC, PC), pl.ds(pl.multiple_of(RES[n] * HD + hm * wide, HD), wide)]
+            dst = backs[n].at[rd(half * PC, PC), pl.ds(pl.multiple_of(RES[n] * HD + hm * wide, HD), wide)]
             fn(src, dst, ssb.at[j, e, n], rsb.at[hm, half, n], cc, zb, own)
 
     def back_got(n):
         wide = G * HD if n < 2 else HD
         for hh in range(4):
             for half in range(2):
-                got(res_ref.at[half * PC:(half + 1) * PC, RES[n] * HD + hh * wide:RES[n] * HD + (hh + 1) * wide], rsb.at[hh, half, n])
-
-    def item(n, e):
+                got(backs[n].at[half * PC:(half + 1) * PC, RES[n] * HD + hh * wide:RES[n] * HD + (hh + 1) * wide], rsb.at[hh, half, n])
+
+    def whose(n):
         t = tile_at(n)
-        j, k, za, ya = owners(t)
+        return t, owners(t)
+
+    def item(at, e):
+        t, (j, k, za, ya) = at
         hi = j >> 1
         half = (e + j) & 1
         same = [za == grp[0], ya == grp[1], half == grp[2]]
@@ -487,23 +500,25 @@
         sends = [k != t_me] + [there[d] & jnp.logical_not(same[d]) for d in range(3)]
         return 2 * t + half, j, slots, there, sends
 
-    def link(n, e, u, slots, r):
+    def link(e, u, slots, r):
         if r == 0:
             return rcopy(dkv.at[u], rb0.at[slots[0]], ss0.at[slots[0]], rs0.at[slots[0]], c, 1 - t_me)
         rb, ss, rs = ((rb1, ss1, rs1), (rb2, ss2, rs2), (rb3, ss3, rs3))[r - 1]
         return rcopy(rb0.at[slots[0]], rb.at[e, slots[r]], ss.at[e, slots[r]], rs.at[e, slots[r]], nbrs[3 - r if e else r - 1], t_me)
 
     def over(n):
+        at = whose(n)
         for e in range(2):
-            u, _, slots, _, sends = item(n, e)
+            u, _, slots, _, sends = item(at, e)
 
             @pl.when(sends[0])
             def _():
-                link(n, e, u, slots, 0).start()
+                link(e, u, slots, 0).start()
 
     def stage(n, r):
+        at = whose(n)
         for e in range(2):
-            u, j, slots, there, sends = item(n, e)
+            u, j, slots, there, sends = item(at, e)
             acc = rb0.at[slots[0]]
 
             @pl.when(there[r])
@@ -525,7 +540,47 @@
             if r < 3:
                 @pl.when(sends[r + 1])
                 def _():
-                    link(n, e, u, slots, r + 1).start()
+                    link(e, u, slots, r + 1).start()
+
+    inner, blocks = wo.shape[0], wo.shape[1] // UQ
+
+    def weights(n, m):
+        slot = m & 1
+        if n:
+            return wq.at[rd(m * UQ, UQ), :], wb.at[slot, :, :inner], lsem.at[n, slot]
+        return wo.at[:, rd(m * UQ, UQ)], wa.at[slot, :inner, :], lsem.at[n, slot]
+
+    def held(m):
+        return s_scr.at[m & 3, :UQ, :]
+
+    def stored(n, m):
+        return pltpu.make_async_copy(held(m), (y_ref, dx_ref)[n].at[:, rd(m * UQ, UQ)], osem.at[m & 3])
+
+    def product(n, m):
+        got(*weights(n, m)[1:])
+
+        @pl.when(m > 3)
+        def _():
+            stored(n, m - 4).wait()
+        w = weights(n, m)[1]
+        held(m)[:, :] = mt(res[:, inner:], w[:, :]) if n else mm(res[:, :inner], w[:, :])
+        stored(n, m).start()
+
+        @pl.when(m + 2 < blocks)
+        def _():
+            pltpu.make_async_copy(*weights(n, m + 2)).start()
+
+    def products(n, m):
+        product(n, 2 * m)
+        product(n, 2 * m + 1)
+
+    def settle(n):
+        for m in range(blocks - 4, blocks):
+            stored(n, m).wait()
+
+    for n in range(2):
+        for m in range(2):
+            pltpu.make_async_copy(*weights(n, m)).start()
 
     def tile_at(n):
         n = jnp.minimum(n, NT - 1)
@@ -616,27 +671,45 @@
     for j in range(4):
         back(send, j, 1)
 
+    late = NT + LAGS[3] - blocks // 2
+
     @each(NT + LAGS[3], NT)
     def _(n):
         sums(n)
 
+        @pl.when(n < NT + blocks // 2)
+        def _():
+            products(0, n - NT)
+
+        @pl.when(n == late)
+        def _():
+            settle(0)
+            back_got(1)
+
+        @pl.when(n >= late)
+        def _():
+            products(1, n - late)
+    settle(1)
+
     @each(NT)
     def _(n):
+        at = whose(n)
         for e in range(2):
-            u, _, slots, _, sends = item(n, e)
+            u, _, slots, _, sends = item(at, e)
             for r in range(4):
                 @pl.when(sends[r])
                 def _():
-                    link(n, e, u, slots, r).wait_send()
-    for n in range(1, 4):
+                    link(e, u, slots, r).wait_send()
+    for n in (2, 3):
         back_got(n)
-        for j in range(4):
+    for j in range(4):
+        for n in (1, 2, 3):
             back(sent, j, n)
 
 
-def attention_kernel(x_ref, dy_ref, wq, wk, wv, wo, res_ref, qo, doo, ko, vo, o, l2, qt, s_scr, acc, *scr):
-    finish = forward(x_ref, dy_ref, wq, wk, wv, wo, qo, doo, ko, vo, o, l2, qt, s_scr, acc, *scr[:18])
-    backward(qo, doo, o, l2, ko, vo, res_ref, qt, s_scr, acc, *scr[18:])
+def attention_kernel(x_ref, dy_ref, wq, wk, wv, wo, kvb_ref, y_ref, dx_ref, qo, doo, ko, vo, o, l2, qt, s_scr, acc, wa, wb, lsem, *scr):
+    finish = forward(x_ref, dy_ref, wq, wk, wv, wo, qo, doo, ko, vo, o, l2, qt, s_scr, acc, wa, wb, lsem, *scr[:15])
+    backward(qo, doo, o, l2, ko, vo, wq, wo, kvb_ref, y_ref, dx_ref, qt, s_scr, acc, wa, wb, lsem, *scr[15:])
     finish()
 
 
@@ -647,17 +720,17 @@
     n, d = x.shape
     wide = vm((4 * UQ, G * HD), BF)
     turned = vm((4 * G, HD, UQ), BF)
-    shared = [wide, wide, vm((S, HD), BF), vm((S, HD), BF), wide, vm((4 * G, UQ), F32), turned, vm((NG, KT, UQ), F32), vm((4 * G, HD, UQ), F32)]
-    fwd = [vm((2 * n, 2 * wk.shape[1] + wq.shape[1]), BF), vm((2 * n, wq.shape[1]), BF), vm((n, d), BF), vm((n, d), BF),
-           vm((2, d, PB), BF), vm((2, PB, d), BF), vm((4 * G, UQ), F32), vm((4 * G, 8, UQ), F32), vm((1, UQ), F32), *both(2), dma((2, 2)),
+    shared = [wide, wide, vm((S, HD), BF), vm((S, HD), BF), wide, vm((4 * G, UQ), F32), turned, vm((NG, KT, UQ), F32), vm((4 * G, HD, UQ), F32),
+              vm((2, d, PB), BF), vm((2, PB, d), BF), dma((2, 2))]
+    fwd = [vm((2 * n, 2 * wk.shape[1] + wq.shape[1]), BF), vm((2 * n, wq.shape[1]), BF), vm((n, d), BF), vm((n, d), BF), vm((4 * G, UQ), F32), vm((4 * G, 8, UQ), F32), vm((1, UQ), F32), *both(2),
            *both(4, 4, 2), *both(8, 8), *both(8, 8)]
-    bwd = [vm((S // UQ, 2, HD, UQ), F32), vm((4 * G, UQ), F32), turned,
+    bwd = [vm((2 * n, 2 * wq.shape[1]), BF), dma((4,)), vm((S // UQ, 2, HD, UQ), F32), vm((4 * G, UQ), F32), turned,
            vm((G, KT, UQ), F32), vm((32, 2, HD, UQ), F32), vm((2, 8, 2, HD, UQ), F32),
            vm((2, 4, 2, HD, UQ), F32), vm((2, 2, 2, HD, UQ), F32), vm((4, 2, UQ, HD), BF), *both(4, 2, 4),
            *both(32), *both(2, 8), *both(2, 4), *both(2, 2)]
     return pl.pallas_call(
         attention_kernel,
-        out_shape=shape((2 * n, 2 * wq.shape[1] + 2 * wk.shape[1]), BF), in_specs=[VM] * 2 + [ANY] * 4, out_specs=VM,
+        out_shape=(shape((2 * n, 2 * wk.shape[1]), BF),) + (shape((2 * n, d), F32),) * 2, in_specs=[VM] * 2 + [ANY] * 4, out_specs=(VM, ANY, ANY),
         scratch_shapes=shared + fwd + bwd, compiler_params=params(65472, 2), name='attention')(x, dy, wq, wk, wv, wo)
 
 
@@ -665,88 +738,74 @@
 DEEP = 4
 
 
-def out_kernel(res_ref, wo, wq, wk, wv, y_own, y_in, dx_own, dx_in, bo, bq, bk, bv, away, lsem, ssem, rsem):
+def out_kernel(kv_ref, y_part, dx_part, wk, wv, y_own, y_in, dx_own, dx_in, bx, bk, bv, away, ysem, lsem, ssem, rsem):
     c, t = lax.axis_index('cp'), lax.axis_index('tp')
     rows, width = y_own.shape
-    blocks = width // NB
+    blocks, depth = width // NB, wk.shape[1]
+    mine, other = rd(t * rows, rows), rd((1 - t) * rows, rows)
 
     def cols(b):
         return rd(b * NB, NB)
 
-    def part(n, wide):
-        return res_ref[:, RES[n] * HD:RES[n] * HD + wide]
-
-    def loads(n, b, fn):
-        s = b % DEEP
-        if n == 0:
-            fn(pltpu.make_async_copy(wo.at[:, cols(b)], bo.at[s], lsem.at[0, s]))
-        else:
-            for m, (w, buf) in enumerate(((wq, bq), (wk, bk), (wv, bv))):
-                fn(pltpu.make_async_copy(w.at[cols(b), :], buf.at[s], lsem.at[1 + m, s]))
-
-    def start(cp):
-        cp.start()
-
-    def wait(cp):
-        cp.wait()
-
-    for n in range(2):
-        for b in range(DEEP):
-            loads(n, b, start)
+    def loads(b, fn):
+        s = b & 3
+        fn(wk.at[cols(b), :], bk.at[s], lsem.at[0, s])
+        fn(wv.at[cols(b), :], bv.at[s], lsem.at[1, s])
+        fn(dx_part.at[other, cols(b)], bx.at[s, :rows, :], lsem.at[2, s])
+        fn(dx_part.at[mine, cols(b)], bx.at[s, rows:, :], lsem.at[3, s])
+
+    def start(*cp):
+        pltpu.make_async_copy(*cp).start()
+
+    def wait(*cp):
+        pltpu.make_async_copy(*cp).wait()
+
+    def part(at):
+        return jnp.concatenate([kv_ref[other, at], kv_ref[mine, at]], 0)
+
+    start(y_part.at[mine, :], y_own, ysem)
+    for b in range(DEEP):
+        loads(b, start)
     bar = pltpu.get_barrier_semaphore()
     pl.semaphore_signal(bar, 1, device_id=dev(c, 1 - t), device_id_type=pl.DeviceIdType.MESH)
     pl.semaphore_wait(bar, 1)
-
-    def swap(n, b):
-        return rcopy(away.at[n, b], (y_in, dx_in)[n].at[:, cols(b)], ssem.at[n, b], rsem.at[n, b], c, 1 - t)
-
-    def block(n, b):
-        s = b % DEEP
-        loads(n, b, wait)
-        if n == 0:
-            r = mm(part(0, bo.shape[1]), bo[s])
-        else:
-            r = mt(part(1, bq.shape[2]), bq[s]) + mt(part(2, bk.shape[2]), bk[s]) + mt(part(3, bv.shape[2]), bv[s])
-
-        own = (y_own, dx_own)[n]
-
-        @pl.when(t == 0)
-        def _():
-            own[:, cols(b)] = r[:rows]
-            away[n, b] = r[rows:]
-
-        @pl.when(t == 1)
-        def _():
-            own[:, cols(b)] = r[rows:]
-            away[n, b] = r[:rows]
-        swap(n, b).start()
+    y_swap = rcopy(y_part.at[other, :], y_in, ssem.at[blocks], rsem.at[blocks], c, 1 - t)
+    y_swap.start()
+
+    def swap(b):
+        return rcopy(away.at[b], dx_in.at[:, cols(b)], ssem.at[b], rsem.at[b], c, 1 - t)
+
+    @each(blocks)
+    def _(b):
+        s = b & 3
+        loads(b, wait)
+        r = mt(part(pl.ds(0, depth)), bk[s]) + mt(part(pl.ds(depth, depth)), bv[s]) + bx[s]
+        away[b] = r[:rows]
+        dx_own[:, cols(b)] = r[rows:]
+        swap(b).start()
 
         @pl.when(b + DEEP < blocks)
         def _():
-            loads(n, b + DEEP, start)
-
-    for n in range(2):
-        @each(blocks)
-        def _(b):
-            block(n, b)
+            loads(b + DEEP, start)
 
     @each(blocks)
     def _(b):
-        swap(0, b).wait()
-        swap(1, b).wait()
-
-
-def outputs(res, wo, wq, wk, wv):
-    n, width = res.shape[0] // 2, wo.shape[1]
+        swap(b).wait()
+    y_swap.wait()
+    wait(y_part.at[mine, :], y_own, ysem)
+
+
+def outputs(kv, y_part, dx_part, wk, wv):
+    n, width = kv.shape[0] // 2, wk.shape[0]
     b = width // NB
     dma = pltpu.SemaphoreType.DMA
     vm = pltpu.VMEM
     f = pl.pallas_call(
         out_kernel, out_shape=(shape((n, width), F32),) * 4, in_specs=[VM] + [HB] * 4, out_specs=(VM,) * 4,
-        scratch_shapes=[vm((DEEP, wo.shape[0], NB), BF), vm((DEEP, NB, wq.shape[1]), BF), vm((DEEP, NB, wk.shape[1]), BF),
-                        vm((DEEP, NB, wv.shape[1]), BF), vm((2, b, n, NB), F32), dma((4, DEEP)), dma((2, b)), dma((2, b))],
+        scratch_shapes=[vm((DEEP, 2 * n, NB), F32), vm((DEEP, NB, wk.shape[1]), BF), vm((DEEP, NB, wk.shape[1]), BF),
+                        vm((b, n, NB), F32), dma, dma((4, DEEP)), dma((b + 1,)), dma((b + 1,))],
         compiler_params=params(46080, 1), name='outputs')
-    y_own, y_in, dx_own, dx_in = f(res, wo, wq, wk, wv)
+    y_own, y_in, dx_own, dx_in = f(kv, y_part, dx_part, wk, wv)
     return (y_own + y_in).astype(BF), (dx_own + dx_in).astype(BF)
 
 
@@ -754,7 +813,7 @@
     row_spec = P(('dp', 'cp', 'tp'), None)
 
     def local_step(x_blk, dy_blk, w_query, w_key, w_value, w_out):
-        res = attention(x_blk, dy_blk, w_query, w_key, w_value, w_out)
-        return outputs(res, w_out, w_query, w_key, w_value)
+        kv, y_part, dx_part = attention(x_blk, dy_blk, w_query, w_key, w_value, w_out)
+        return outputs(kv, y_part, dx_part, w_key, w_value)
 
     return jax.shard_map(local_step, mesh=mesh, in_specs=(row_spec, row_spec, P(None, 'tp'), P(None, 'tp'), P(None, 'tp'), P('tp', None)), out_specs=(row_spec, row_spec), check_vma=False)

time: 213 us -> 210 us (0.986)
    pallas_call x2, Pallas kernels: 208 us -> 206 us  [the longest x1 197 us: attention(): pl.pallas_call(attention_kernel, out_shape=(shape((2 * n, 2 * wk.shape[1]...]
where the time goes in v4:
time: 210 us; the launch traced here: 209 us
  Pallas kernels  206 us (98%)
    pallas_call x1, Pallas kernels, attention(): pl.pallas_call(attention_kernel, out_shape=(shape((2 * n, 2 * wk.shape[1]...  197 us
    pallas_call x1, Pallas kernels, outputs(): y_own, y_in, dx_own, dx_in = f(kv, y_part, dx_part, wk, wv)  8.22 us

profile of v4, /device:TPU:1, one launch (start us, length us, event | category | flops | bytes accessed | tf_op | source)
XLA Modules:
  0.0 208.7 jit_solution(16978032445412717182)
XLA Ops:
  0.6 197.3 %attention.1 = (bf16[256,1024]{1,0:T(8,128)(2,1)}, f32[256,3072]{1,0:T(8,128)}, f32[256,3072]{1,0:T(8,128)}) custom-call(bf16[128,3072]{1,0:T(8,128)(2,1)} %x_ref.1, bf16[128,3072]{1,0:T(8,128)(2,1)} %dy_ref.1, bf16[3072,1536]{1,0:T(8,128)(2,1)} %wq.1, bf16[3072,512]{1,0:T(8,128)(2,1)} %wk.3, bf16[3072,512]{1,0:T(8,128)(2,1)} %wv.3, bf16[1536,3072]{1,0:T(8,128)(2,1)} %wo.1), custom_call_target="tpu_custom_call" | custom-call | tf_op jit(solution)/shard_map/attention/pallas_call | solution.py:731
  197.9 0.0 copy-start
  197.9 1.0 copy-done
  199.0 8.2 %outputs.1 = (f32[128,3072]{1,0:T(8,128)S(1)}, f32[128,3072]{1,0:T(8,128)S(1)}, f32[128,3072]{1,0:T(8,128)S(1)}, f32[128,3072]{1,0:T(8,128)S(1)}) custom-call(bf16[256,1024]{1,0:T(8,128)(2,1)S(1)} %copy-done, f32[256,3072]{1,0:T(8,128)} %get-tuple-element.10.y_part, f32[256,3072]{1,0:T(8,128)} %get-tuple-element.11.dx_part, bf16[3072,512]{1,0:T(8,128)(2,1)} %wk.3, ...), custom_call_target="tpu_custom_call" | custom-call | tf_op jit(solution)/shard_map/outputs/pallas_call | solution.py:808
  207.2 1.5 add_convert_fusion
Async XLA Ops:
  197.9 1.0 copy-start

commit v5 on v4

--- a/solution.py
+++ b/solution.py
@@ -484,6 +484,9 @@
         t = tile_at(n)
         return t, owners(t)
 
+    def full(t):
+        return t < NT - 4
+
     def item(at, e):
         t, (j, k, za, ya) = at
         hi = j >> 1
@@ -498,6 +501,8 @@
         for d in range(3):
             there.append(there[d] & same[d])
         sends = [k != t_me] + [there[d] & jnp.logical_not(same[d]) for d in range(3)]
+        if not e:
+            sends[1] = sends[1] & full(t)
         return 2 * t + half, j, slots, there, sends
 
     def link(e, u, slots, r):
@@ -521,7 +526,7 @@
             u, j, slots, there, sends = item(at, e)
             acc = rb0.at[slots[0]]
 
-            @pl.when(there[r])
+            @pl.when(there[r] & full(at[0]) if r == 1 and not e else there[r])
             def _():
                 if r == 0:
                     got(acc, rs0.at[slots[0]])

time: 210 us -> 210 us (level)
  no operation moved by 1% of the time
where the time goes in v5:
time: 210 us; the launch traced here: 209 us
  Pallas kernels  205 us (98%)
    pallas_call x1, Pallas kernels, attention(): pl.pallas_call(attention_kernel, out_shape=(shape((2 * n, 2 * wk.shape[1]...  197 us
    pallas_call x1, Pallas kernels, outputs(): y_own, y_in, dx_own, dx_in = f(kv, y_part, dx_part, wk, wv)  8.26 us

profile of v5, /device:TPU:1, one launch (start us, length us, event | category | flops | bytes accessed | tf_op | source)
XLA Modules:
  0.0 208.6 jit_solution(5369189468614235624)
XLA Ops:
  0.6 197.2 %attention.1 = (bf16[256,1024]{1,0:T(8,128)(2,1)}, f32[256,3072]{1,0:T(8,128)}, f32[256,3072]{1,0:T(8,128)}) custom-call(bf16[128,3072]{1,0:T(8,128)(2,1)} %x_ref.1, bf16[128,3072]{1,0:T(8,128)(2,1)} %dy_ref.1, bf16[3072,1536]{1,0:T(8,128)(2,1)} %wq.1, bf16[3072,512]{1,0:T(8,128)(2,1)} %wk.3, bf16[3072,512]{1,0:T(8,128)(2,1)} %wv.3, bf16[1536,3072]{1,0:T(8,128)(2,1)} %wo.1), custom_call_target="tpu_custom_call" | custom-call | tf_op jit(solution)/shard_map/attention/pallas_call | solution.py:736
  197.8 0.0 copy-start
  197.8 1.0 copy-done
  198.8 8.3 %outputs.1 = (f32[128,3072]{1,0:T(8,128)S(1)}, f32[128,3072]{1,0:T(8,128)S(1)}, f32[128,3072]{1,0:T(8,128)S(1)}, f32[128,3072]{1,0:T(8,128)S(1)}) custom-call(bf16[256,1024]{1,0:T(8,128)(2,1)S(1)} %copy-done, f32[256,3072]{1,0:T(8,128)} %get-tuple-element.10.y_part, f32[256,3072]{1,0:T(8,128)} %get-tuple-element.11.dx_part, bf16[3072,512]{1,0:T(8,128)(2,1)} %wk.3, ...), custom_call_target="tpu_custom_call" | custom-call | tf_op jit(solution)/shard_map/outputs/pallas_call | solution.py:813
  207.1 1.5 add_convert_fusion
Async XLA Ops:
  197.8 1.0 copy-start
